TPU v7x, 128 devices: a 2x2x16 block of a 8x8x16 slice. The times are simulated.
128 devices in a mesh: groups: 4 (over x, y), freq: 16 (over z), mgrp: 2 (over core).
Axes of the slice: x: 2, y: 2, z: 16, core: 2. Of those that a mesh axis runs over, the one named last changes fastest.
The devices are a block of a 8x8x16 slice.
Arguments:
- seeds: int32 [128, 1024], P('groups', 'mgrp'), parts along dimension 0, may hold values from 0 to 1073741823
- noise_amp: float32 [1024, 512], P(('groups', 'freq')), parts along dimension 0, may hold values from 0.3 to 3
- singular_projection: bfloat16 [128, 256, 16, 512], P('groups', 'freq'), parts along dimension 0, may hold values from -0.25 to 0.25
- kl_vecs: bfloat16 [128, 1536, 4096], P(('groups', 'freq'), 'mgrp'), parts along dimension 0, may hold values from -0.09375 to 0.09375
- m_order: int32 [128], P('groups'), parts along dimension 0, may hold values from 0 to 31, each once
- mode_counts: int32 [128], P('groups'), parts along dimension 0, may hold values from 384 to 1536, as said below
Outputs:
- kl_coeffs: bfloat16 [128, 1536, 1024], P(('groups', 'freq'), None, 'mgrp'), parts along dimension 0
There are 4 independent parts, one for each index of `groups`. A program takes and returns all parts, laid end to end along the dimension named above; each array names one. Nothing has to cross between parts.
Inputs may be any that keep to these rules, and one draw needn't show every extreme that they name: `m_order`: each m appears in exactly one slot. `mode_counts`: some m keeps all 1536 modes.
All inputs are finite; a program needn't handle non-finite values.
Results may differ from a plain program's by a relative error of at most 0.0058.
Values may be sent and summed in bfloat16 or wider, within the bound.
No kernel may reach another device: no remote copies, remote signals or barrier semaphores. Data moves between devices by JAX's collectives and lax.ppermute only.
A program may use at most 192 MiB of HBM per device.

v0:
```python
import jax
import jax.numpy as jnp
from jax import lax
from jax.sharding import PartitionSpec as P

golden = 1640531527


def scramble(hashed_seed):
    hashed_seed = hashed_seed ^ hashed_seed >> 16 & 65535
    hashed_seed = hashed_seed * 2146121005
    hashed_seed = hashed_seed ^ hashed_seed >> 15 & 131071
    hashed_seed = hashed_seed * 1863026059
    hashed_seed = hashed_seed ^ hashed_seed >> 16 & 65535
    return ((hashed_seed & 65535).astype(jnp.float32) - 32767.5) / 18918.0


def per_device(seeds, noise_amp, singular_projection, kl_vecs, m_order, mode_counts):
    freq_count = lax.axis_size("freq")
    freq_index = lax.axis_index("freq")
    local_chan = singular_projection.shape[1]
    modes_chan = singular_projection.shape[2]
    baseline_pairs = singular_projection.shape[3]
    batch_groups = kl_vecs.shape[0]
    half_reals = seeds.shape[1]
    order_grid = m_order.reshape(freq_count, batch_groups)
    global_channel = freq_index * local_chan + jnp.arange(local_chan, dtype=jnp.int32)
    channel_index = (
        global_channel[:, None] * baseline_pairs
        + jnp.arange(baseline_pairs, dtype=jnp.int32)[None, :]
    )
    every_m = jnp.arange(m_order.shape[0], dtype=jnp.int32)

    def project(m_number):
        weights = lax.dynamic_index_in_dim(singular_projection, m_number, 0, keepdims=False)
        seed_row = lax.dynamic_index_in_dim(seeds, m_number, 0, keepdims=False)
        noise_draw = scramble(seed_row[None, None, :] + channel_index[:, :, None] * golden)
        visible = (noise_amp[:, :, None] * noise_draw).astype(jnp.bfloat16)
        stacked = jnp.einsum("fkb,fbr->fkr", weights, visible, preferred_element_type=jnp.float32)
        return stacked.astype(jnp.bfloat16).reshape(local_chan * modes_chan, half_reals)

    outputs = []
    for batch_index in range(batch_groups):
        m_numbers = order_grid[:, batch_index]
        grouped = lax.map(jax.vmap(project), m_numbers.reshape(-1, 4))
        outgoing = grouped.reshape(m_numbers.shape[0], local_chan * modes_chan, half_reals)
        arrived = lax.all_to_all(outgoing, "freq", split_axis=0, concat_axis=1, tiled=True)
        vectors = arrived[0]
        position_index = freq_index * batch_groups + batch_index
        kept_m_number = jnp.sum(jnp.where(every_m == position_index, m_order, 0))
        kept_limit = jnp.sum(jnp.where(every_m == kept_m_number, mode_counts, 0))
        eigen_panel = kl_vecs[batch_index]
        coeffs = jnp.dot(
            lax.all_gather(eigen_panel, "mgrp", axis=0, tiled=True),
            vectors,
            preferred_element_type=jnp.float32,
        )
        row_index = jnp.arange(coeffs.shape[0], dtype=jnp.int32)
        outputs.append(jnp.where(row_index[:, None] < kept_limit, coeffs, 0.0).astype(jnp.bfloat16))
    return jnp.stack(outputs, 0)


def solution(mesh):
    placed = (
        P("groups", "mgrp"),
        P(("groups", "freq"), None),
        P("groups", "freq", None, None),
        P(("groups", "freq"), "mgrp", None),
        P("groups"),
        P("groups"),
    )
    return jax.shard_map(
        per_device,
        mesh=mesh,
        in_specs=placed,
        out_specs=P(("groups", "freq"), None, "mgrp"),
        check_vma=False,
    )
```

profile of v0, /device:TPU:214, one launch (start us, length us, event | category | flops | bytes accessed | tf_op | source)
XLA Modules:
  0.0 576.5 jit_solution(3924146653526477834)
XLA Ops:
  10.4 152.2 %while.27 = (s32[]{:T(128)}, bf16[4,4,256,512]{3,2,1,0:T(8,128)(2,1)}, s32[4,4]{1,0:T(4,128)S(1)}, bf16[32,16,16,512]{3,2,1,0:T(8,128)(2,1)}, s32[32,512]{1,0:T(...) while((s32[]{:T(128)}, bf16[4,4,256,512]{3,2,1,0:T(8,128)(2,1)}, ...), condition=%wide.region_7.8_spmd.clone, body=%wide.region_6.7_spmd.clone.sunk | while | flops 822632448 | bytes 6480165 | solution.py:45
  10.5 4.0 gather_fusion.2
  16.7 30.7 %fusion.82 = bf16[4,16,16,512]{3,2,1,0:T(8,128)(2,1)S(1)} fusion(bf16[4,16,16,512]{3,2,1,0:T(8,128)(2,1)S(1)} %gather_fusion.2, s32[4,512]{1,0:T(4,128)S(1)} %gather_fusion.3, f32[16,512]{1,0:T(8,128)S(1)} %broadcast_multiply_fusion.5, s32[16,512]{1,0:T(8,128)S(1)} %add_multiply_fusion.6), kind=kOutput, calls=%fused_computation.41.clone.1 | convolution fusion | flops 822607872 | bytes 2170880 | tf_op jit(solution)/shard_map/while/body/eval_jaxpr/vmap(fkb,fbr->fkr)/dot_general | solution.py:39
  48.5 4.0 gather_fusion.2
  54.8 30.7 %fusion.82 = bf16[4,16,16,512]{3,2,1,0:T(8,128)(2,1)S(1)} fusion(bf16[4,16,16,512]{3,2,1,0:T(8,128)(2,1)S(1)} %gather_fusion.2, s32[4,512]{1,0:T(4,128)S(1)} %gather_fusion.3, f32[16,512]{1,0:T(8,128)S(1)} %broadcast_multiply_fusion.5, s32[16,512]{1,0:T(8,128)S(1)} %add_multiply_fusion.6), kind=kOutput, calls=%fused_computation.41.clone.1 | convolution fusion | flops 822607872 | bytes 2170880 | tf_op jit(solution)/shard_map/while/body/eval_jaxpr/vmap(fkb,fbr->fkr)/dot_general | solution.py:39
  86.5 4.0 gather_fusion.2
  92.8 30.7 %fusion.82 = bf16[4,16,16,512]{3,2,1,0:T(8,128)(2,1)S(1)} fusion(bf16[4,16,16,512]{3,2,1,0:T(8,128)(2,1)S(1)} %gather_fusion.2, s32[4,512]{1,0:T(4,128)S(1)} %gather_fusion.3, f32[16,512]{1,0:T(8,128)S(1)} %broadcast_multiply_fusion.5, s32[16,512]{1,0:T(8,128)S(1)} %add_multiply_fusion.6), kind=kOutput, calls=%fused_computation.41.clone.1 | convolution fusion | flops 822607872 | bytes 2170880 | tf_op jit(solution)/shard_map/while/body/eval_jaxpr/vmap(fkb,fbr->fkr)/dot_general | solution.py:39
  124.6 4.0 gather_fusion.2
  130.9 30.7 %fusion.82 = bf16[4,16,16,512]{3,2,1,0:T(8,128)(2,1)S(1)} fusion(bf16[4,16,16,512]{3,2,1,0:T(8,128)(2,1)S(1)} %gather_fusion.2, s32[4,512]{1,0:T(4,128)S(1)} %gather_fusion.3, f32[16,512]{1,0:T(8,128)S(1)} %broadcast_multiply_fusion.5, s32[16,512]{1,0:T(8,128)S(1)} %add_multiply_fusion.6), kind=kOutput, calls=%fused_computation.41.clone.1 | convolution fusion | flops 822607872 | bytes 2170880 | tf_op jit(solution)/shard_map/while/body/eval_jaxpr/vmap(fkb,fbr->fkr)/dot_general | solution.py:39
  162.6 16.6 %all-to-all-start.1 = ((bf16[16,256,512]{2,1,0:T(8,128)(2,1)}), bf16[16,256,512]{2,1,0:T(8,128)(2,1)}, u32[]{:S(2)}, u32[]{:S(2)}) async-start(bf16[16,256,512]{2,1,0:T(8,128)(2,1)} %bitcast.63), calls=%async_computation.1 | async-start | bytes 8388608 | tf_op jit(solution)/shard_map/all_to_all | solution.py:47
  179.4 10.5 %fusion.66 = (bf16[1,768,4096]{2,1,0:T(8,128)(2,1)}, bf16[1,768,4096]{2,1,0:T(8,128)(2,1)}) fusion(bf16[2,768,4096]{2,1,0:T(8,128)(2,1)} %param.13), kind=kLoop, calls=%fused_computation.80 | loop fusion | bytes 25165824 | tf_op jit(solution)/shard_map/slice | solution.py:52
  192.3 145.7 %while.26 = (s32[]{:T(128)}, bf16[4,4,256,512]{3,2,1,0:T(8,128)(2,1)}, s32[4,4]{1,0:T(4,128)S(1)}, bf16[32,16,16,512]{3,2,1,0:T(8,128)(2,1)}, s32[32,512]{1,0:T(...) while((s32[]{:T(128)}, bf16[4,4,256,512]{3,2,1,0:T(8,128)(2,1)}, ...), condition=%wide.region_3.4_spmd.clone, body=%wide.region_2.3_spmd.clone.sunk | while | flops 822632448 | bytes 6480165 | solution.py:45
  192.3 4.0 gather_fusion
  197.0 30.7 %fusion.79 = bf16[4,16,16,512]{3,2,1,0:T(8,128)(2,1)S(1)} fusion(bf16[4,16,16,512]{3,2,1,0:T(8,128)(2,1)S(1)} %gather_fusion, s32[4,512]{1,0:T(4,128)S(1)} %gather_fusion.1, f32[16,512]{1,0:T(8,128)S(1)} %broadcast_multiply_fusion.4, s32[16,512]{1,0:T(8,128)S(1)} %add_multiply_fusion.5), kind=kOutput, calls=%fused_computation.16.clone.1 | convolution fusion | flops 822607872 | bytes 2170880 | tf_op jit(solution)/shard_map/while/body/eval_jaxpr/vmap(fkb,fbr->fkr)/dot_general | solution.py:39
  228.7 4.0 gather_fusion
  233.4 30.7 %fusion.79 = bf16[4,16,16,512]{3,2,1,0:T(8,128)(2,1)S(1)} fusion(bf16[4,16,16,512]{3,2,1,0:T(8,128)(2,1)S(1)} %gather_fusion, s32[4,512]{1,0:T(4,128)S(1)} %gather_fusion.1, f32[16,512]{1,0:T(8,128)S(1)} %broadcast_multiply_fusion.4, s32[16,512]{1,0:T(8,128)S(1)} %add_multiply_fusion.5), kind=kOutput, calls=%fused_computation.16.clone.1 | convolution fusion | flops 822607872 | bytes 2170880 | tf_op jit(solution)/shard_map/while/body/eval_jaxpr/vmap(fkb,fbr->fkr)/dot_general | solution.py:39
  269.9 30.7 %fusion.79 = bf16[4,16,16,512]{3,2,1,0:T(8,128)(2,1)S(1)} fusion(bf16[4,16,16,512]{3,2,1,0:T(8,128)(2,1)S(1)} %gather_fusion, s32[4,512]{1,0:T(4,128)S(1)} %gather_fusion.1, f32[16,512]{1,0:T(8,128)S(1)} %broadcast_multiply_fusion.4, s32[16,512]{1,0:T(8,128)S(1)} %add_multiply_fusion.5), kind=kOutput, calls=%fused_computation.16.clone.1 | convolution fusion | flops 822607872 | bytes 2170880 | tf_op jit(solution)/shard_map/while/body/eval_jaxpr/vmap(fkb,fbr->fkr)/dot_general | solution.py:39
  306.3 30.7 %fusion.79 = bf16[4,16,16,512]{3,2,1,0:T(8,128)(2,1)S(1)} fusion(bf16[4,16,16,512]{3,2,1,0:T(8,128)(2,1)S(1)} %gather_fusion, s32[4,512]{1,0:T(4,128)S(1)} %gather_fusion.1, f32[16,512]{1,0:T(8,128)S(1)} %broadcast_multiply_fusion.4, s32[16,512]{1,0:T(8,128)S(1)} %add_multiply_fusion.5), kind=kOutput, calls=%fused_computation.16.clone.1 | convolution fusion | flops 822607872 | bytes 2170880 | tf_op jit(solution)/shard_map/while/body/eval_jaxpr/vmap(fkb,fbr->fkr)/dot_general | solution.py:39
  338.1 24.3 %all-to-all-done.1 = bf16[16,256,512]{2,1,0:T(8,128)(2,1)} async-done(((bf16[16,256,512]{2,1,0:T(8,128)(2,1)}), bf16[16,256,512]{2,1,0:T(8,128)(2,1)}, u32[]{:S(2)}, u32[]{:S(2)}) %all-to-all-start.1) | async-done | bytes 4194336 | tf_op jit(solution)/shard_map/all_to_all | solution.py:47
  362.4 9.8 %all-to-all-start = ((bf16[16,256,512]{2,1,0:T(8,128)(2,1)}), bf16[16,256,512]{2,1,0:T(8,128)(2,1)}, u32[]{:S(2)}, u32[]{:S(2)}) async-start(bf16[16,256,512]{2,1,0:T(8,128)(2,1)} %bitcast.62), calls=%async_computation | async-start | bytes 8388608 | tf_op jit(solution)/shard_map/all_to_all | solution.py:47
  376.8 11.9 %fusion.59 = bf16[1,1536,512]{1,2,0:T(8,128)(2,1)} fusion(bf16[4096,512]{1,0:T(8,128)(2,1)} %bitcast.6, bf16[1,1536,4096]{2,1,0:T(8,128)(2,1)} %all-gather.7.cloned.1.call-done, pred[1536]{0:T(1024)(128)(4,1)S(1)} %get-tuple-element.255), kind=kOutput, calls=%fused_computation.66 | convolution fusion | flops 6444023808 | bytes 18351616 | tf_op jit(solution)/shard_map/dot_general | solution.py:53
  388.7 18.8 %all-gather.5.cloned.1.call-done = bf16[1,1536,4096]{2,1,0:T(8,128)(2,1)} async-done(((bf16[1,768,4096]{2,1,0:T(8,128)(2,1)}), bf16[1,1536,4096]{2,1,0:T(8,128)(2,1)}) %all-gather.5.cloned.1.call-update) | async-done | bytes 12582928 | tf_op jit(solution)/shard_map/all_gather | solution.py:54
  407.5 147.9 %all-to-all-done = bf16[16,256,512]{2,1,0:T(8,128)(2,1)} async-done(((bf16[16,256,512]{2,1,0:T(8,128)(2,1)}), bf16[16,256,512]{2,1,0:T(8,128)(2,1)}, u32[]{:S(2)}, u32[]{:S(2)}) %all-to-all-start) | async-done | bytes 4194336 | tf_op jit(solution)/shard_map/all_to_all | solution.py:47
  555.4 11.1 %fusion.56 = bf16[1,1536,512]{1,2,0:T(8,128)(2,1)S(1)} fusion(bf16[4096,512]{1,0:T(8,128)(2,1)} %bitcast.1, bf16[1,1536,4096]{2,1,0:T(8,128)(2,1)} %all-gather.5.cloned.1.call-done, pred[1536]{0:T(1024)(128)(4,1)S(1)} %get-tuple-element.256), kind=kOutput, calls=%fused_computation.65 | convolution fusion | flops 6444023808 | bytes 18351616 | tf_op jit(solution)/shard_map/dot_general | solution.py:53
  (71 shorter events, 42.4 us)
Async XLA Ops:
  162.6 199.8 %all-to-all-start.1 = ((bf16[16,256,512]{2,1,0:T(8,128)(2,1)}), bf16[16,256,512]{2,1,0:T(8,128)(2,1)}, u32[]{:S(2)}, u32[]{:S(2)}) async-start(bf16[16,256,512]{2,1,0:T(8,128)(2,1)} %bitcast.63), calls=%async_computation.1 | async-start | bytes 8388608 | tf_op jit(solution)/shard_map/all_to_all | solution.py:47
  179.3 10.6 %copy-start.4 = (s32[16]{0:T(128)S(1)}, s32[16]{0:T(128)}, u32[]{:S(2)}) copy-start(s32[16]{0:T(128)} %get-tuple-element.219) | copy-start | bytes 196
  179.3 13.1 %copy-start = (s32[32,512]{1,0:T(8,128)S(1)}, s32[32,512]{1,0:T(8,128)}, u32[]{:S(2)}) copy-start(s32[32,512]{1,0:T(8,128)} %get-tuple-element.402) | copy-start | bytes 196612
  179.3 13.0 %copy-start.1 = (f32[16,512]{1,0:T(8,128)S(1)}, f32[16,512]{1,0:T(8,128)}, u32[]{:S(2)}) copy-start(f32[16,512]{1,0:T(8,128)} %get-tuple-element.403) | copy-start | bytes 98308
  179.3 197.5 %all-gather.7.cloned.1.call-start = ((), (), s32[]{:S(2)}) async-start(), calls=%async_computation.3 | async-start | bytes 18874368 | tf_op jit(solution)/shard_map/all_gather | solution.py:54
  338.1 34.9 %copy-start.3 = (s32[32]{0:T(128)S(1)}, s32[32]{0:T(128)}, u32[]{:S(2)}) copy-start(s32[32]{0:T(128)} %param.14) | copy-start | bytes 388
  338.1 35.6 %copy-start.5 = (s32[32]{0:T(128)S(1)}, s32[32]{0:T(128)}, u32[]{:S(2)}) copy-start(s32[32]{0:T(128)} %param.15) | copy-start | bytes 388
  362.4 193.0 %all-to-all-start = ((bf16[16,256,512]{2,1,0:T(8,128)(2,1)}), bf16[16,256,512]{2,1,0:T(8,128)(2,1)}, u32[]{:S(2)}, u32[]{:S(2)}) async-start(bf16[16,256,512]{2,1,0:T(8,128)(2,1)} %bitcast.62), calls=%async_computation | async-start | bytes 8388608 | tf_op jit(solution)/shard_map/all_to_all | solution.py:47
  372.2 35.3 %all-gather.5.cloned.1.call-start = ((), (), s32[]{:S(2)}) async-start(), calls=%async_computation.2 | async-start | bytes 18874368 | tf_op jit(solution)/shard_map/all_gather | solution.py:54
  555.4 11.1 %copy-start.2 = (bf16[1,1536,512]{1,2,0:T(8,128)(2,1)S(1)}, bf16[1,1536,512]{1,2,0:T(8,128)(2,1)}, u32[]{:S(2)}) copy-start(bf16[1,1536,512]{1,2,0:T(8,128)(2,1)} %fusion.59) | copy-start | bytes 4718596
Sparse Core Ops, SparseCore 0:
  190.0 32.7 all-gather.6
  374.7 32.7 all-gather.4
where the time goes:
time: 577 us; the launch traced here: 576 us
  matrix products  268 us (46%)
  waiting for transfers between devices  192 us (33%)
  local copies, waits for them, and re-layouts  68.1 us (12%)
  starting transfers between devices  26.7 us (5%)
  between operations  13.5 us (2%)
  other arithmetic  7.8 us (1%)
    dot_general x8, matrix products, project(): jnp.einsum('fkb,fbr->fkr', weights, visible, preferred_element_type=jnp.f...  245 us
    all_to_all x2, waiting for transfers between devices, per_device(): lax.all_to_all(outgoing, 'freq', split_axis=0, concat_axis=1, tiled=True)  172 us
    gather x8, local copies, waits for them, and re-layouts, project(): lax.dynamic_index_in_dim(singular_projection, m_number, 0, keepdims=False)  32 us
    all_to_all x2, starting transfers between devices, per_device(): lax.all_to_all(outgoing, 'freq', split_axis=0, concat_axis=1, tiled=True)  26.4 us
    dot_general x2, matrix products, per_device(): jnp.dot(lax.all_gather(eigen_panel, 'mgrp', axis=0, tiled=True), vectors,...  23 us
    all_gather x2, waiting for transfers between devices, per_device(): lax.all_gather(eigen_panel, 'mgrp', axis=0, tiled=True)  18.9 us
  transfers between devices with their start and end apart: 4, of which 3 were waited for; matrix products, arithmetic and copies ran while one was open for 30% of the time, Pallas kernels for 0%

commit v1 on v0

v1 whole, which is shorter than its diff:
```python
import functools

import jax
import jax.numpy as jnp
from jax import lax
from jax.experimental import pallas as pl
from jax.experimental.pallas import tpu as pltpu
from jax.sharding import PartitionSpec as P

golden = 1640531527
tile = 256


def wrap(value):
    value &= 0xFFFFFFFF
    return value - (1 << 32) if value >= 1 << 31 else value


def in_order(vmem=None):
    return pltpu.CompilerParams(
        dimension_semantics=("arbitrary",), vmem_limit_bytes=None if vmem is None else vmem * 2**20
    )


def draw_bits(x):
    x = x ^ lax.shift_right_logical(x, 16)
    x = x * 2146121005
    x = x ^ lax.shift_right_logical(x, 15)
    x = x * 1863026059
    x = x ^ lax.shift_right_logical(x, 16)
    return (x & 65535).astype(jnp.float32)


def pick_body(order_ref, ids_ref, seeds_ref, own_ref, sent_ref):
    first = 2 * ids_ref[0]
    own_ref[...] = jnp.broadcast_to(seeds_ref[pl.ds(order_ref[first + ids_ref[1]], 1), :], own_ref.shape)
    sent_ref[...] = jnp.broadcast_to(seeds_ref[pl.ds(order_ref[first + 1 - ids_ref[1]], 1), :], sent_ref.shape)


def pick(m_order, ids, seeds):
    rows = jax.ShapeDtypeStruct((8, seeds.shape[1]), seeds.dtype)
    smem = pl.BlockSpec(memory_space=pltpu.SMEM)
    vmem = pl.BlockSpec(memory_space=pltpu.VMEM)
    return pl.pallas_call(
        pick_body, out_shape=[rows, rows], in_specs=[smem, smem, vmem], out_specs=[vmem, vmem], name="pick"
    )(m_order, ids, seeds)


def weigh_body(order_ref, ids_ref, amp_ref, *refs):
    out_ref = refs[-1]
    for place, w_ref in enumerate(refs[:-1]):
        for chan in range(w_ref.shape[1]):
            scale = amp_ref[chan : chan + 1, :] * (1.0 / 18918.0)
            out_ref[place, chan] = (w_ref[0, chan].astype(jnp.float32) * scale).astype(jnp.bfloat16)


def weigh(m_order, ids, singular_projection, noise_amp, part, chan):
    modes, pairs = singular_projection.shape[2:]
    count = m_order.shape[0] // 2
    each = 4

    def rows_of(place):
        return pl.BlockSpec(
            (1, chan, modes, pairs), lambda i, m, ids: (m[2 * (each * i + place) + ids[1]], part, 0, 0)
        )

    return pl.pallas_call(
        weigh_body,
        out_shape=jax.ShapeDtypeStruct((count, chan, modes, pairs), jnp.bfloat16),
        grid_spec=pltpu.PrefetchScalarGridSpec(
            num_scalar_prefetch=2,
            grid=(count // each,),
            in_specs=[pl.BlockSpec((chan, pairs), lambda i, m, ids: (part, 0))] + [rows_of(k) for k in range(each)],
            out_specs=pl.BlockSpec((each, chan, modes, pairs), lambda i, m, ids: (i, 0, 0, 0)),
        ),
        compiler_params=in_order(),
        name="weigh",
    )(m_order, ids, noise_amp, *[singular_projection] * each)


def draw_tiles(seed_refs, channel, pairs):
    base = (lax.broadcasted_iota(jnp.int32, (8, tile), 0) + channel * pairs) * golden
    held = seed_refs[0].shape[1]
    for r0 in range(0, held * len(seed_refs), tile):
        start = seed_refs[r0 // held][:, r0 % held : r0 % held + tile] + base
        for b0 in range(0, pairs, tile):
            bits = jnp.concatenate([draw_bits(start + wrap(b * golden)) for b in range(b0, b0 + tile, 8)], 0)
            yield r0, b0, bits.astype(jnp.bfloat16)


def channel_of(place, half, chan):
    return place // chan * (2 * chan) + half * chan + place % chan


def centre_of(w):
    return 32767.5 * jnp.sum(w.astype(jnp.float32), axis=1, keepdims=True)


def put_product(w, draws, r0, b0, pairs, total, centre, out_ref, place):
    piece = jnp.dot(w[:, b0 : b0 + tile], draws, preferred_element_type=jnp.float32)
    total = piece if b0 == 0 else total + piece
    if b0 + tile == pairs:
        out_ref[place, :, r0 : r0 + tile] = (total - centre).astype(jnp.bfloat16)
    return total


def seed_spec(seeds):
    return pl.BlockSpec(seeds.shape, lambda i: (0, 0))


def draw_body(own_ref, far_ref, out_ref, *, first, half, chan):
    each, pairs = out_ref.shape[:2]
    for place in range(each):
        channel = channel_of(first + pl.program_id(0) * each + place, half, chan)
        for r0, b0, draws in draw_tiles((own_ref, far_ref), channel, pairs):
            out_ref[place, b0 : b0 + tile, r0 : r0 + tile] = draws


def draw(seeds, first, count, half, chan, pairs, each):
    reals = sum(s.shape[1] for s in seeds)
    return pl.pallas_call(
        functools.partial(draw_body, first=first, half=half, chan=chan),
        out_shape=jax.ShapeDtypeStruct((count, pairs, reals), jnp.bfloat16),
        grid=(count // each,),
        in_specs=[seed_spec(s) for s in seeds],
        out_specs=pl.BlockSpec((each, pairs, reals), lambda i: (i, 0, 0)),
        compiler_params=in_order(32),
        name="draw",
    )(*seeds)


def project_body(own_ref, far_ref, w_ref, out_ref, *, first, half, chan):
    each, _, pairs = w_ref.shape
    for place in range(each):
        channel = channel_of(first + pl.program_id(0) * each + place, half, chan)
        w = w_ref[place]
        centre = centre_of(w)
        total = None
        for r0, b0, draws in draw_tiles((own_ref, far_ref), channel, pairs):
            total = put_product(w, draws, r0, b0, pairs, total, centre, out_ref, place)


def project(seeds, weights, first, count, half, chan, each):
    modes, pairs = weights.shape[1:]
    reals = sum(s.shape[1] for s in seeds)
    return pl.pallas_call(
        functools.partial(project_body, first=first, half=half, chan=chan),
        out_shape=jax.ShapeDtypeStruct((count, modes, reals), jnp.bfloat16),
        grid=(count // each,),
        in_specs=[seed_spec(s) for s in seeds]
        + [pl.BlockSpec((each, modes, pairs), lambda i: (first // each + i, 0, 0))],
        out_specs=pl.BlockSpec((each, modes, reals), lambda i: (i, 0, 0)),
        compiler_params=in_order(),
        name="project",
    )(*seeds, weights)


def finish_body(own_ref, far_ref, w_ref, held_ref, held_w_ref, out_ref, held_out_ref, *, first, half, chan):
    each, _, pairs = w_ref.shape
    held_each = held_ref.shape[0] // each
    for place in range(each):
        channel = channel_of(first + pl.program_id(0) * each + place, half, chan)
        w = w_ref[place]
        centre = centre_of(w)
        kept = range(place * held_each, (place + 1) * held_each)
        held_w = [held_w_ref[k] for k in kept]
        held_centre = [centre_of(one) for one in held_w]
        total = None
        held_total = [None] * held_each
        for r0, b0, draws in draw_tiles((own_ref, far_ref), channel, pairs):
            total = put_product(w, draws, r0, b0, pairs, total, centre, out_ref, place)
            for n, k in enumerate(kept):
                old = held_ref[k, b0 : b0 + tile, r0 : r0 + tile]
                held_total[n] = put_product(
                    held_w[n], old, r0, b0, pairs, held_total[n], held_centre[n], held_out_ref, k
                )


def finish(seeds, weights, held, half, chan, each):
    modes, pairs = weights.shape[1:]
    reals = sum(s.shape[1] for s in seeds)
    first = held.shape[0]
    count = weights.shape[0] - first
    steps = count // each
    held_each = first // steps
    return pl.pallas_call(
        functools.partial(finish_body, first=first, half=half, chan=chan),
        out_shape=[
            jax.ShapeDtypeStruct((count, modes, reals), jnp.bfloat16),
            jax.ShapeDtypeStruct((first, modes, reals), jnp.bfloat16),
        ],
        grid=(steps,),
        in_specs=[seed_spec(s) for s in seeds]
        + [
            pl.BlockSpec((each, modes, pairs), lambda i: (first // each + i, 0, 0)),
            pl.BlockSpec((held_each, pairs, reals), lambda i: (i, 0, 0)),
            pl.BlockSpec((held_each, modes, pairs), lambda i: (i, 0, 0)),
        ],
        out_specs=[
            pl.BlockSpec((each, modes, reals), lambda i: (i, 0, 0)),
            pl.BlockSpec((held_each, modes, reals), lambda i: (i, 0, 0)),
        ],
        compiler_params=in_order(48),
        name="finish",
    )(*seeds, weights, held, weights)


def transform_body(ids_ref, order_ref, counts_ref, near_ref, far_ref, lead_ref, early_ref, last_ref, out_ref, sum_ref, *, cut):
    step = pl.program_id(0)
    held = near_ref.shape[1]

    @pl.when(step == 0)
    def _():
        sum_ref[...] = jnp.zeros(sum_ref.shape, sum_ref.dtype)

    trail = jnp.where(step < cut, early_ref[...], last_ref[...])
    vectors = jnp.concatenate([lead_ref[...], trail], 0)
    for place, kl_ref in enumerate((near_ref, far_ref)):
        sum_ref[place] += jnp.dot(kl_ref[0], vectors, preferred_element_type=jnp.float32)

    @pl.when(step == pl.num_programs(0) - 1)
    def _():
        limit = counts_ref[order_ref[2 * ids_ref[0] + ids_ref[1]]]
        for place in range(2):
            first = (ids_ref[1] if place == 0 else 1 - ids_ref[1]) * held
            first = pl.multiple_of(first, held)
            row = first + lax.broadcasted_iota(jnp.int32, sum_ref.shape[1:], 0)
            coeffs = jnp.where(row < limit, sum_ref[place], 0.0).astype(jnp.bfloat16)
            out_ref[0, pl.ds(first, held), :] = coeffs


def transform(ids, m_order, mode_counts, kl_near, kl_far, vectors, rows, half, halves, slots):
    held, length = kl_near.shape[1:]
    reals = vectors[0].shape[1] // halves
    cut = vectors[1].shape[0] // rows

    def kl_rows(i, s, o, c):
        return (s[1], 0, i)

    return pl.pallas_call(
        functools.partial(transform_body, cut=cut),
        out_shape=jax.ShapeDtypeStruct((slots, 2 * held, reals), jnp.bfloat16),
        grid_spec=pltpu.PrefetchScalarGridSpec(
            num_scalar_prefetch=3,
            grid=(length // (2 * rows),),
            in_specs=[
                pl.BlockSpec((1, held, 2 * rows), kl_rows),
                pl.BlockSpec((1, held, 2 * rows), kl_rows),
                pl.BlockSpec((rows, reals), lambda i, s, o, c: (i, half)),
                pl.BlockSpec((rows, reals), lambda i, s, o, c: (jnp.minimum(i, cut - 1), half)),
                pl.BlockSpec((rows, reals), lambda i, s, o, c: (jnp.maximum(i - cut, 0), half)),
            ],
            out_specs=pl.BlockSpec((1, 2 * held, reals), lambda i, s, o, c: (s[1] * (slots - 1), 0, 0)),
            scratch_shapes=[pltpu.VMEM((2, held, reals), jnp.float32)],
        ),
        compiler_params=in_order(32),
        name="transform",
    )(ids, m_order, mode_counts, kl_near, kl_far, *vectors)


def per_device(seeds, noise_amp, singular_projection, kl_vecs, m_order, mode_counts):
    d = lax.axis_index("freq")
    core = lax.axis_index("mgrp")
    modes, pairs = singular_projection.shape[2:]
    chan = singular_projection.shape[1] // 2
    ids = jnp.stack([d, core]).astype(jnp.int32)
    swap = [(0, 1), (1, 0)]

    own_seeds, sent_seeds = pick(m_order, ids, seeds)
    far_seeds = lax.ppermute(sent_seeds, "mgrp", swap)

    def exchange(sent):
        return lax.all_to_all(sent, "freq", split_axis=0, concat_axis=0, tiled=True).reshape(-1, modes, pairs)

    sent = weigh(m_order, ids, singular_projection, noise_amp, 0, chan)
    sent, far_seeds, kl_sent = lax.optimization_barrier((sent, far_seeds, kl_vecs))
    both_seeds = (own_seeds, far_seeds)
    weights = exchange(sent)
    kl_far = lax.ppermute(kl_sent, "mgrp", swap)
    total = weights.shape[0]
    ahead = total * 3 // 4
    held = draw(both_seeds, 0, ahead, 1, chan, pairs, 4)
    late_order, held = lax.optimization_barrier((m_order, held))
    late_weights = exchange(weigh(late_order, ids, singular_projection, noise_amp, 1, chan))
    first = project(both_seeds, weights, 0, total, 0, chan, 4)
    last, early = finish(both_seeds, late_weights, held, 1, chan, 2)

    vectors = [v.reshape(-1, v.shape[2]) for v in (first, early, last)]
    rows = chan * modes
    sent = transform(ids, m_order, mode_counts, kl_vecs, kl_far, vectors, rows, 1, 2, 1)
    got = lax.ppermute(sent, "mgrp", swap)
    kept = transform(ids, m_order, mode_counts, kl_vecs, kl_far, vectors, rows, 0, 2, 2)
    return lax.dynamic_update_slice_in_dim(kept, got, 1 - core, 0)


def solution(mesh):
    placed = (
        P("groups", "mgrp"),
        P(("groups", "freq"), None),
        P("groups", "freq", None, None),
        P(("groups", "freq"), "mgrp", None),
        P("groups"),
        P("groups"),
    )
    return jax.shard_map(
        per_device,
        mesh=mesh,
        in_specs=placed,
        out_specs=P(("groups", "freq"), None, "mgrp"),
        check_vma=False,
    )
```

time: 577 us -> 333 us (0.58)
  Pallas kernels: 0 us -> 272 us
  matrix products: 268 us -> 0 us
  waiting for transfers between devices: 192 us -> 11.5 us
  local copies, waits for them, and re-layouts: 68.1 us -> 18.8 us
  between operations: 13.5 us -> 0.15 us
  other arithmetic: 7.8 us -> 0.66 us
    pallas_call x0 -> x8, Pallas kernels: none -> 272 us  [the longest x1 106 us: project(): pl.pallas_call(functools.partial(project_body, first=first, half=half, ch...]
    dot_general x10 -> x0, matrix products: 268 us -> none  [the longest x8 245 us: project(): jnp.einsum('fkb,fbr->fkr', weights, visible, preferred_element_type=jnp.f...]
    all_to_all x2, waiting for transfers between devices: 172 us -> 11.4 us  [exchange(): lax.all_to_all(sent, 'freq', split_axis=0, concat_axis=0, tiled=True)]
    gather x16 -> x0, local copies, waits for them, and re-layouts: 40 us -> none  [the longest x8 32 us: project(): lax.dynamic_index_in_dim(singular_projection, m_number, 0, keepdims=False)]
    all_gather x2 -> x0, waiting for transfers between devices: 18.9 us -> none  [per_device(): lax.all_gather(eigen_panel, 'mgrp', axis=0, tiled=True)]
    unnamed x12 -> x32, local copies, waits for them, and re-layouts: 0.03 us -> 16.2 us
    slice x2 -> x0, local copies, waits for them, and re-layouts: 11.2 us -> none  [the longest x1 10.5 us: per_device(): eigen_panel = kl_vecs[batch_index]]
    another operation x5 -> x0, local copies, waits for them, and re-layouts: 7.65 us -> none
  transfers between devices with their start and end apart: 4 -> 5, of which waited for: 3 -> 1; matrix products, arithmetic and copies ran while one was open for 30% -> 0% of each run, Pallas kernels for 0% -> 77%
where the time goes in v1:
time: 333 us; the launch traced here: 330 us
  Pallas kernels  272 us (82%)
  starting transfers between devices  26.2 us (8%)
  local copies, waits for them, and re-layouts  18.8 us (6%)
  waiting for transfers between devices  11.5 us (3%)
    pallas_call x1, Pallas kernels, project(): pl.pallas_call(functools.partial(project_body, first=first, half=half, ch...  106 us
    pallas_call x1, Pallas kernels, draw(): pl.pallas_call(functools.partial(draw_body, first=first, half=half, chan=...  77.9 us
    pallas_call x1, Pallas kernels, finish(): pl.pallas_call(functools.partial(finish_body, first=first, half=half, cha...  44.7 us
    pallas_call x2, Pallas kernels, transform(): pl.pallas_call(functools.partial(transform_body, cut=cut), out_shape=jax....  33.1 us
    all_to_all x2, starting transfers between devices, exchange(): lax.all_to_all(sent, 'freq', split_axis=0, concat_axis=0, tiled=True)  26.1 us
    unnamed x32, local copies, waits for them, and re-layouts  16.2 us
    all_to_all x2, waiting for transfers between devices, exchange(): lax.all_to_all(sent, 'freq', split_axis=0, concat_axis=0, tiled=True)  11.4 us
    pallas_call x2, Pallas kernels, weigh(): pl.pallas_call(weigh_body, out_shape=jax.ShapeDtypeStruct((count, chan, m...  9.29 us
  transfers between devices with their start and end apart: 5, of which 1 were waited for; matrix products, arithmetic and copies ran while one was open for 0% of the time, Pallas kernels for 77%

profile of v1, /device:TPU:214, one launch (start us, length us, event | category | flops | bytes accessed | tf_op | source)
XLA Modules:
  0.0 329.5 jit_solution(11260618378081457432)
XLA Ops:
  0.0 0.7 pad_add_fusion.ids_ref
  0.7 1.5 pick.1
  2.1 4.6 %weigh.2 = bf16[16,8,16,512]{3,2,1,0:T(8,128)(2,1)} custom-call(s32[32]{0:T(128)} %order_ref.8, s32[2]{0:T(128)} %pad_add_fusion.ids_ref, f32[16,512]{1,0:T(8,128)} %amp_ref.3, bf16[32,16,16,512]{3,2,1,0:T(8,128)(2,1)} %refs_3_.3, bf16[32,16,16,512]{3,2,1,0:T(8,128)(2,1)} %refs_3_.3, bf16[32,16,16,512]{3,2,1,0:T(8,128)(2,1)} %refs_3_.3, ...), custom_call_target="tpu_custom_call" | custom-call | tf_op jit(solution)/shard_map/weigh/pallas_call | solution.py:67
  6.8 16.7 %all-to-all-start = ((bf16[16,8,16,512]{3,2,1,0:T(8,128)(2,1)}), bf16[16,8,16,512]{3,2,1,0:T(8,128)(2,1)S(1)}, u32[]{:S(2)}, u32[]{:S(2)}) async-start(bf16[16,8,16,512]{3,2,1,0:T(8,128)(2,1)} %weigh.2), calls=%async_computation | async-start | bytes 4194304 | tf_op jit(solution)/shard_map/all_to_all | solution.py:273
  23.4 0.0 collective-permute-start.1
  23.5 77.9 %draw.1.held_ref = bf16[96,512,1024]{2,1,0:T(8,128)(2,1)} custom-call(s32[8,512]{1,0:T(8,128)S(1)} %copy-done.8, s32[8,512]{1,0:T(8,128)S(1)} %collective-permute-done.far_ref), custom_call_target="tpu_custom_call" | custom-call | tf_op jit(solution)/shard_map/draw/pallas_call | solution.py:121
  101.4 4.6 %weigh.3 = bf16[16,8,16,512]{3,2,1,0:T(8,128)(2,1)} custom-call(s32[32]{0:T(128)} %order_ref.8, s32[2]{0:T(128)} %pad_add_fusion.ids_ref, f32[16,512]{1,0:T(8,128)} %amp_ref.3, bf16[32,16,16,512]{3,2,1,0:T(8,128)(2,1)} %refs_3_.3, bf16[32,16,16,512]{3,2,1,0:T(8,128)(2,1)} %refs_3_.3, bf16[32,16,16,512]{3,2,1,0:T(8,128)(2,1)} %refs_3_.3, ...), custom_call_target="tpu_custom_call" | custom-call | tf_op jit(solution)/shard_map/weigh/pallas_call | solution.py:67
  106.0 11.4 %all-to-all-done = bf16[16,8,16,512]{3,2,1,0:T(8,128)(2,1)S(1)} async-done(((bf16[16,8,16,512]{3,2,1,0:T(8,128)(2,1)}), bf16[16,8,16,512]{3,2,1,0:T(8,128)(2,1)S(1)}, u32[]{:S(2)}, u32[]{:S(2)}) %all-to-all-start) | async-done | bytes 2097184 | tf_op jit(solution)/shard_map/all_to_all | solution.py:273
  117.5 1.3 copy-done.15
  118.8 9.5 %all-to-all-start.1 = ((bf16[16,8,16,512]{3,2,1,0:T(8,128)(2,1)}), bf16[16,8,16,512]{3,2,1,0:T(8,128)(2,1)S(1)}, u32[]{:S(2)}, u32[]{:S(2)}) async-start(bf16[16,8,16,512]{3,2,1,0:T(8,128)(2,1)} %weigh.3), calls=%async_computation.1 | async-start | bytes 4194304 | tf_op jit(solution)/shard_map/all_to_all | solution.py:273
  128.3 105.8 %project.1 = bf16[128,16,1024]{2,1,0:T(8,128)(2,1)} custom-call(s32[8,512]{1,0:T(8,128)} %get-tuple-element.16.own_ref, s32[8,512]{1,0:T(8,128)} %copy-done.10, bf16[128,16,512]{2,1,0:T(8,128)(2,1)} %bitcast.15), custom_call_target="tpu_custom_call" | custom-call | tf_op jit(solution)/shard_map/project/pallas_call | solution.py:146
  234.1 0.0 copy-start.12
  234.2 0.0 copy-start.14
  234.2 44.7 %finish.1 = (bf16[32,16,1024]{2,1,0:T(8,128)(2,1)S(1)}, bf16[96,16,1024]{2,1,0:T(8,128)(2,1)}) custom-call(s32[8,512]{1,0:T(8,128)S(1)} %copy-done.9, s32[8,512]{1,0:T(8,128)S(1)} %copy-done.11, bf16[128,16,512]{2,1,0:T(8,128)(2,1)S(1)} %bitcast.9, bf16[96,512,1024]{2,1,0:T(8,128)(2,1)} %draw.1.held_ref, bf16[128,16,512]{2,1,0:T(8,128)(2,1)S(1)} %bitcast.10), custom_call_target="tpu_custom_call" | custom-call | tf_op jit(solution)/shard_map/finish/pallas_call | solution.py:186
  279.0 0.0 copy-start
  279.0 4.9 %copy-done = bf16[2,768,4096]{2,1,0:T(8,128)(2,1)S(1)} copy-done((bf16[2,768,4096]{2,1,0:T(8,128)(2,1)S(1)}, bf16[2,768,4096]{2,1,0:T(8,128)(2,1)}, u32[]{:S(2)}) %copy-start) | copy-done | bytes 12582936
  283.9 1.9 copy-done.4
  285.8 16.7 %transform.3 = bf16[1,1536,512]{2,1,0:T(8,128)(2,1)} custom-call(s32[2]{0:T(128)S(1)} %copy-done.13, s32[32]{0:T(128)S(1)} %copy-done.12, s32[32]{0:T(128)S(1)} %copy-done.14, bf16[2,768,4096]{2,1,0:T(8,128)(2,1)S(1)} %copy-done, bf16[2,768,4096]{2,1,0:T(8,128)(2,1)} %collective-permute-done.1.far_ref, bf16[2048,1024]{1,0:T(8,128)(2,1)S(1)} %bitcast.7, ...), custom_call_target="tpu_custom_call" | custom-call | tf_op jit(solution)/shard_map/transform/pallas_call | solution.py:240
  302.5 0.0 copy-start.1
  302.5 4.6 %copy-done.1 = bf16[2,768,4096]{2,1,0:T(8,128)(2,1)S(1)} copy-done((bf16[2,768,4096]{2,1,0:T(8,128)(2,1)S(1)}, bf16[2,768,4096]{2,1,0:T(8,128)(2,1)}, u32[]{:S(2)}) %copy-start.1) | copy-done | bytes 12582936
  307.1 2.2 copy-done.3
  309.3 1.2 copy-done.7
  310.5 16.4 %transform.2 = bf16[2,1536,512]{2,1,0:T(8,128)(2,1)} custom-call(s32[2]{0:T(128)S(1)} %copy-done.13, s32[32]{0:T(128)S(1)} %copy-done.12, s32[32]{0:T(128)S(1)} %copy-done.14, bf16[2,768,4096]{2,1,0:T(8,128)(2,1)S(1)} %copy-done.1, bf16[2,768,4096]{2,1,0:T(8,128)(2,1)} %collective-permute-done.1.far_ref, bf16[2048,1024]{1,0:T(8,128)(2,1)S(1)} %bitcast.8, ...), custom_call_target="tpu_custom_call" | custom-call | tf_op jit(solution)/shard_map/transform/pallas_call | solution.py:240
  326.9 2.7 constant_dynamic-update-slice_fusion
  (28 shorter events, 0.1 us)
Async XLA Ops:
  2.1 4.7 %collective-permute-start = (s32[8,512]{1,0:T(8,128)}, s32[8,512]{1,0:T(8,128)S(1)}, u32[]{:S(2)}, u32[]{:S(2)}) collective-permute-start(s32[8,512]{1,0:T(8,128)} %get-tuple-element.14), channel_id=1, source_target_pairs={{0,1},{1,0},{2,3},{3,2},{4,5},{5,4},{6,7},{7,6},{8,9},{9,8},{10,11... | collective-permute-start | bytes 49160 | tf_op jit(solution)/shard_map/ppermute | solution.py:270
  6.8 16.7 %copy-start.8 = (s32[8,512]{1,0:T(8,128)S(1)}, s32[8,512]{1,0:T(8,128)}, u32[]{:S(2)}) copy-start(s32[8,512]{1,0:T(8,128)} %get-tuple-element.16.own_ref) | copy-start | bytes 49156
  6.8 94.6 %copy-start.10 = (s32[8,512]{1,0:T(8,128)}, s32[8,512]{1,0:T(8,128)S(1)}, u32[]{:S(2)}) copy-start(s32[8,512]{1,0:T(8,128)S(1)} %collective-permute-done.far_ref) | copy-start | bytes 49156
  6.8 110.7 %all-to-all-start = ((bf16[16,8,16,512]{3,2,1,0:T(8,128)(2,1)}), bf16[16,8,16,512]{3,2,1,0:T(8,128)(2,1)S(1)}, u32[]{:S(2)}, u32[]{:S(2)}) async-start(bf16[16,8,16,512]{3,2,1,0:T(8,128)(2,1)} %weigh.2), calls=%async_computation | async-start | bytes 4194304 | tf_op jit(solution)/shard_map/all_to_all | solution.py:273
  23.4 255.5 %collective-permute-start.1 = (bf16[2,768,4096]{2,1,0:T(8,128)(2,1)}, bf16[2,768,4096]{2,1,0:T(8,128)(2,1)}, u32[]{:S(2)}, u32[]{:S(2)}) collective-permute-start(bf16[2,768,4096]{2,1,0:T(8,128)(2,1)} %near_ref.3), channel_id=1, source_target_pairs={{0,1},{1,0},{2,3},{3,2},{4,5},{5,4},{6,7},{7,6},{8,9},{9,8},{10,11... | collective-permute-start | bytes 37748744 | tf_op jit(solution)/shard_map/ppermute | solution.py:279
  117.5 1.3 copy-start.15
  118.8 115.3 %all-to-all-start.1 = ((bf16[16,8,16,512]{3,2,1,0:T(8,128)(2,1)}), bf16[16,8,16,512]{3,2,1,0:T(8,128)(2,1)S(1)}, u32[]{:S(2)}, u32[]{:S(2)}) async-start(bf16[16,8,16,512]{3,2,1,0:T(8,128)(2,1)} %weigh.3), calls=%async_computation.1 | async-start | bytes 4194304 | tf_op jit(solution)/shard_map/all_to_all | solution.py:273
  128.3 105.8 %copy-start.9 = (s32[8,512]{1,0:T(8,128)S(1)}, s32[8,512]{1,0:T(8,128)}, u32[]{:S(2)}) copy-start(s32[8,512]{1,0:T(8,128)} %get-tuple-element.16.own_ref) | copy-start | bytes 49156
  128.3 105.8 %copy-start.11 = (s32[8,512]{1,0:T(8,128)S(1)}, s32[8,512]{1,0:T(8,128)}, u32[]{:S(2)}) copy-start(s32[8,512]{1,0:T(8,128)} %copy-done.10) | copy-start | bytes 49156
  234.1 44.8 %copy-start.2 = (bf16[128,16,1024]{2,1,0:T(8,128)(2,1)S(1)}, bf16[128,16,1024]{2,1,0:T(8,128)(2,1)}, u32[]{:S(2)}) copy-start(bf16[128,16,1024]{2,1,0:T(8,128)(2,1)} %project.1) | copy-start | bytes 12582916
  234.1 44.8 %copy-start.12 = (s32[32]{0:T(128)S(1)}, s32[32]{0:T(128)}, u32[]{:S(2)}) copy-start(s32[32]{0:T(128)} %order_ref.8) | copy-start | bytes 388
  234.2 44.8 %copy-start.13 = (s32[2]{0:T(128)S(1)}, s32[2]{0:T(128)}, u32[]{:S(2)}) copy-start(s32[2]{0:T(128)} %pad_add_fusion.ids_ref) | copy-start | bytes 28
  234.2 44.8 %copy-start.14 = (s32[32]{0:T(128)S(1)}, s32[32]{0:T(128)}, u32[]{:S(2)}) copy-start(s32[32]{0:T(128)} %counts_ref.3) | copy-start | bytes 388
  278.9 23.6 %copy-start.6 = (bf16[32,16,1024]{2,1,0:T(8,128)(2,1)}, bf16[32,16,1024]{2,1,0:T(8,128)(2,1)S(1)}, u32[]{:S(2)}) copy-start(bf16[32,16,1024]{2,1,0:T(8,128)(2,1)S(1)} %get-tuple-element.22) | copy-start | bytes 3145732
  279.0 4.9 %copy-start = (bf16[2,768,4096]{2,1,0:T(8,128)(2,1)S(1)}, bf16[2,768,4096]{2,1,0:T(8,128)(2,1)}, u32[]{:S(2)}) copy-start(bf16[2,768,4096]{2,1,0:T(8,128)(2,1)} %near_ref.3) | copy-start | bytes 37748740
  283.9 1.9 copy-start.4
  285.8 16.7 %copy-start.5 = (bf16[96,16,1024]{2,1,0:T(8,128)(2,1)S(1)}, bf16[96,16,1024]{2,1,0:T(8,128)(2,1)}, u32[]{:S(2)}) copy-start(bf16[96,16,1024]{2,1,0:T(8,128)(2,1)} %get-tuple-element.21) | copy-start | bytes 9437188
  302.5 24.4 %collective-permute-start.2 = (bf16[1,1536,512]{2,1,0:T(8,128)(2,1)}, bf16[1,1536,512]{2,1,0:T(8,128)(2,1)}, u32[]{:S(2)}, u32[]{:S(2)}) collective-permute-start(bf16[1,1536,512]{2,1,0:T(8,128)(2,1)} %transform.3), channel_id=1, source_target_pairs={{0,1},{1,0},{2,3},{3,2},{4,5},{5,4},{6,7},{7,6},{8,9},{9,8},{10,11... | collective-permute-start | bytes 4718600 | tf_op jit(solution)/shard_map/ppermute | solution.py:291
  302.5 4.6 %copy-start.1 = (bf16[2,768,4096]{2,1,0:T(8,128)(2,1)S(1)}, bf16[2,768,4096]{2,1,0:T(8,128)(2,1)}, u32[]{:S(2)}) copy-start(bf16[2,768,4096]{2,1,0:T(8,128)(2,1)} %near_ref.3) | copy-start | bytes 37748740
  307.1 2.2 copy-start.3
  309.3 1.2 copy-start.7

commit v2 on v1

--- a/solution.py
+++ b/solution.py
@@ -6,6 +6,7 @@
 from jax.experimental import pallas as pl
 from jax.experimental.pallas import tpu as pltpu
 from jax.sharding import PartitionSpec as P
+
 
 golden = 1640531527
 tile = 256
@@ -124,15 +125,17 @@
         grid=(count // each,),
         in_specs=[seed_spec(s) for s in seeds],
         out_specs=pl.BlockSpec((each, pairs, reals), lambda i: (i, 0, 0)),
-        compiler_params=in_order(32),
+        compiler_params=in_order(60),
         name="draw",
     )(*seeds)
 
 
-def project_body(own_ref, far_ref, w_ref, out_ref, *, first, half, chan):
+def project_body(ids_ref, own_ref, far_ref, w_ref, *refs, half, chan, local):
+    out_ref = refs[-1]
     each, _, pairs = w_ref.shape
+    block = block_of(pl.program_id(0), ids_ref, chan // each, local)
     for place in range(each):
-        channel = channel_of(first + pl.program_id(0) * each + place, half, chan)
+        channel = channel_of(block * each + place, half, chan)
         w = w_ref[place]
         centre = centre_of(w)
         total = None
@@ -140,19 +143,43 @@
             total = put_product(w, draws, r0, b0, pairs, total, centre, out_ref, place)
 
 
-def project(seeds, weights, first, count, half, chan, each):
-    modes, pairs = weights.shape[1:]
+def block_of(step, ids, blocks, local):
+    if local:
+        return ids[0] * blocks + step
+    chip = step // blocks
+    return (chip + (chip >= ids[0]).astype(jnp.int32)) * blocks + step % blocks
+
+
+def project(ids, seeds, weights, vectors, half, chan, each, local):
+    count, modes, pairs = weights.shape
     reals = sum(s.shape[1] for s in seeds)
-    return pl.pallas_call(
-        functools.partial(project_body, first=first, half=half, chan=chan),
+    blocks = chan // each
+    steps = blocks if local else count // each - blocks
+
+    def at(i, ids):
+        return (block_of(i, ids, blocks, local), 0, 0)
+
+    operands = [ids, *seeds, weights]
+    in_specs = [pl.BlockSpec(s.shape, lambda i, ids: (0, 0)) for s in seeds]
+    in_specs += [pl.BlockSpec((each, modes, pairs), at)]
+    aliases = {}
+    if vectors is not None:
+        aliases = {len(operands): 0}
+        operands.append(vectors)
+        in_specs.append(pl.BlockSpec(memory_space=pl.ANY))
+    return pl.pallas_call(
+        functools.partial(project_body, half=half, chan=chan, local=local),
         out_shape=jax.ShapeDtypeStruct((count, modes, reals), jnp.bfloat16),
-        grid=(count // each,),
-        in_specs=[seed_spec(s) for s in seeds]
-        + [pl.BlockSpec((each, modes, pairs), lambda i: (first // each + i, 0, 0))],
-        out_specs=pl.BlockSpec((each, modes, reals), lambda i: (i, 0, 0)),
-        compiler_params=in_order(),
-        name="project",
-    )(*seeds, weights)
+        grid_spec=pltpu.PrefetchScalarGridSpec(
+            num_scalar_prefetch=1,
+            grid=(steps,),
+            in_specs=in_specs,
+            out_specs=pl.BlockSpec((each, modes, reals), at),
+        ),
+        input_output_aliases=aliases,
+        compiler_params=in_order(60),
+        name="near" if local else "project",
+    )(*operands)
 
 
 def finish_body(own_ref, far_ref, w_ref, held_ref, held_w_ref, out_ref, held_out_ref, *, first, half, chan):
@@ -200,60 +227,68 @@
             pl.BlockSpec((each, modes, reals), lambda i: (i, 0, 0)),
             pl.BlockSpec((held_each, modes, reals), lambda i: (i, 0, 0)),
         ],
-        compiler_params=in_order(48),
+        compiler_params=in_order(60),
         name="finish",
     )(*seeds, weights, held, weights)
 
 
-def transform_body(ids_ref, order_ref, counts_ref, near_ref, far_ref, lead_ref, early_ref, last_ref, out_ref, sum_ref, *, cut):
+def transform_body(ids_ref, order_ref, counts_ref, near_ref, far_ref, *refs, rows, blocks, modes):
+    vec_refs, out_ref = refs[:-1], refs[-1]
     step = pl.program_id(0)
-    held = near_ref.shape[1]
-
-    @pl.when(step == 0)
+    first = step * rows
+    limit = counts_ref[order_ref[2 * ids_ref[0] + ids_ref[1]]]
+    mine = step // blocks == ids_ref[1]
+
+    def run(kl_ref):
+        total = None
+        lead, *trail = vec_refs
+        at = [(ref, k) for ref in trail for k in range(0, ref.shape[0], modes)]
+        for k, (ref, start) in enumerate(at):
+            piece = jnp.concatenate([lead[k * modes : (k + 1) * modes, :], ref[start : start + modes, :]], 0)
+            part = jnp.dot(kl_ref[0, :, 2 * k * modes : 2 * (k + 1) * modes], piece, preferred_element_type=jnp.float32)
+            total = part if total is None else total + part
+        row = first + lax.broadcasted_iota(jnp.int32, total.shape, 0)
+        out_ref[0] = jnp.where(row < limit, total, 0.0).astype(jnp.bfloat16)
+
+    @pl.when((first < limit) & mine)
     def _():
-        sum_ref[...] = jnp.zeros(sum_ref.shape, sum_ref.dtype)
-
-    trail = jnp.where(step < cut, early_ref[...], last_ref[...])
-    vectors = jnp.concatenate([lead_ref[...], trail], 0)
-    for place, kl_ref in enumerate((near_ref, far_ref)):
-        sum_ref[place] += jnp.dot(kl_ref[0], vectors, preferred_element_type=jnp.float32)
-
-    @pl.when(step == pl.num_programs(0) - 1)
+        run(near_ref)
+
+    @pl.when((first < limit) & jnp.logical_not(mine))
     def _():
-        limit = counts_ref[order_ref[2 * ids_ref[0] + ids_ref[1]]]
-        for place in range(2):
-            first = (ids_ref[1] if place == 0 else 1 - ids_ref[1]) * held
-            first = pl.multiple_of(first, held)
-            row = first + lax.broadcasted_iota(jnp.int32, sum_ref.shape[1:], 0)
-            coeffs = jnp.where(row < limit, sum_ref[place], 0.0).astype(jnp.bfloat16)
-            out_ref[0, pl.ds(first, held), :] = coeffs
-
-
-def transform(ids, m_order, mode_counts, kl_near, kl_far, vectors, rows, half, halves, slots):
+        run(far_ref)
+
+    @pl.when(first >= limit)
+    def _():
+        out_ref[...] = jnp.zeros(out_ref.shape, out_ref.dtype)
+
+
+def transform(ids, m_order, mode_counts, kl_near, kl_far, vectors, modes, half, halves, slots):
     held, length = kl_near.shape[1:]
     reals = vectors[0].shape[1] // halves
-    cut = vectors[1].shape[0] // rows
-
-    def kl_rows(i, s, o, c):
-        return (s[1], 0, i)
-
-    return pl.pallas_call(
-        functools.partial(transform_body, cut=cut),
+    rows = 256
+    blocks = held // rows
+
+    def near(i, s, o, c):
+        return (s[1], jnp.clip(i - s[1] * blocks, 0, blocks - 1), 0)
+
+    def far(i, s, o, c):
+        return (s[1], jnp.clip(i - (1 - s[1]) * blocks, 0, blocks - 1), 0)
+
+    return pl.pallas_call(
+        functools.partial(transform_body, rows=rows, blocks=blocks, modes=modes),
         out_shape=jax.ShapeDtypeStruct((slots, 2 * held, reals), jnp.bfloat16),
         grid_spec=pltpu.PrefetchScalarGridSpec(
             num_scalar_prefetch=3,
-            grid=(length // (2 * rows),),
+            grid=(2 * blocks,),
             in_specs=[
-                pl.BlockSpec((1, held, 2 * rows), kl_rows),
-                pl.BlockSpec((1, held, 2 * rows), kl_rows),
-                pl.BlockSpec((rows, reals), lambda i, s, o, c: (i, half)),
-                pl.BlockSpec((rows, reals), lambda i, s, o, c: (jnp.minimum(i, cut - 1), half)),
-                pl.BlockSpec((rows, reals), lambda i, s, o, c: (jnp.maximum(i - cut, 0), half)),
+                pl.BlockSpec((1, rows, length), near),
+                pl.BlockSpec((1, rows, length), far),
+                *[pl.BlockSpec((v.shape[0], reals), lambda i, s, o, c: (0, half)) for v in vectors],
             ],
-            out_specs=pl.BlockSpec((1, 2 * held, reals), lambda i, s, o, c: (s[1] * (slots - 1), 0, 0)),
-            scratch_shapes=[pltpu.VMEM((2, held, reals), jnp.float32)],
+            out_specs=pl.BlockSpec((1, rows, reals), lambda i, s, o, c: (s[1] * (slots - 1), i, 0)),
         ),
-        compiler_params=in_order(32),
+        compiler_params=in_order(60),
         name="transform",
     )(ids, m_order, mode_counts, kl_near, kl_far, *vectors)
 
@@ -277,12 +312,12 @@
     both_seeds = (own_seeds, far_seeds)
     weights = exchange(sent)
     kl_far = lax.ppermute(kl_sent, "mgrp", swap)
-    total = weights.shape[0]
-    ahead = total * 3 // 4
+    ahead = weights.shape[0] * 3 // 4
     held = draw(both_seeds, 0, ahead, 1, chan, pairs, 4)
-    late_order, held = lax.optimization_barrier((m_order, held))
+    near = project(ids, both_seeds, sent.reshape(-1, modes, pairs), None, 0, chan, 4, True)
+    late_order, held, near = lax.optimization_barrier((m_order, held, near))
     late_weights = exchange(weigh(late_order, ids, singular_projection, noise_amp, 1, chan))
-    first = project(both_seeds, weights, 0, total, 0, chan, 4)
+    first = project(ids, both_seeds, weights, near, 0, chan, 8, False)
     last, early = finish(both_seeds, late_weights, held, 1, chan, 2)
 
     vectors = [v.reshape(-1, v.shape[2]) for v in (first, early, last)]

time: 333 us -> 443 us (1.33)
  waiting for transfers between devices: 11.5 us -> 144 us
  local copies, waits for them, and re-layouts: 18.8 us -> 1.84 us
  Pallas kernels: 272 us -> 264 us
    all_to_all x2, waiting for transfers between devices: 11.4 us -> 144 us  [exchange(): lax.all_to_all(sent, 'freq', split_axis=0, concat_axis=0, tiled=True)]
    unnamed x32 -> x4, local copies, waits for them, and re-layouts: 16.2 us -> 0.6 us
    pallas_call x3 -> x4, Pallas kernels: 139 us -> 130 us  [the longest x2 107 us: project(): pl.pallas_call(functools.partial(project_body, half=half, chan=chan, loca...]
  transfers between devices with their start and end apart: 5 -> 5, of which waited for: 1 -> 2; matrix products, arithmetic and copies ran while one was open for 0% -> 0% of each run, Pallas kernels for 77% -> 36%
where the time goes in v2:
time: 443 us; the launch traced here: 436 us
  Pallas kernels  264 us (60%)
  waiting for transfers between devices  144 us (33%)
  starting transfers between devices  26.2 us (6%)
    all_to_all x2, waiting for transfers between devices, exchange(): lax.all_to_all(sent, 'freq', split_axis=0, concat_axis=0, tiled=True)  144 us
    pallas_call x2, Pallas kernels, project(): pl.pallas_call(functools.partial(project_body, half=half, chan=chan, loca...  107 us
    pallas_call x1, Pallas kernels, draw(): pl.pallas_call(functools.partial(draw_body, first=first, half=half, chan=...  78.7 us
    pallas_call x1, Pallas kernels, finish(): pl.pallas_call(functools.partial(finish_body, first=first, half=half, cha...  44.8 us
    all_to_all x2, starting transfers between devices, exchange(): lax.all_to_all(sent, 'freq', split_axis=0, concat_axis=0, tiled=True)  26.1 us
    pallas_call x2, Pallas kernels, transform(): pl.pallas_call(functools.partial(transform_body, rows=rows, blocks=blocks...  23.1 us
    pallas_call x2, Pallas kernels, weigh(): pl.pallas_call(weigh_body, out_shape=jax.ShapeDtypeStruct((count, chan, m...  9.29 us
  transfers between devices with their start and end apart: 5, of which 2 were waited for; matrix products, arithmetic and copies ran while one was open for 0% of the time, Pallas kernels for 36%

profile of v2, /device:TPU:214, one launch (start us, length us, event | category | flops | bytes accessed | tf_op | source)
XLA Modules:
  0.0 436.4 jit_solution(10485258538317591747)
XLA Ops:
  0.0 0.6 pad_add_fusion.ids_ref
  0.6 1.5 pick.1
  2.1 0.0 collective-permute-start
  2.1 4.6 %weigh.2 = bf16[16,8,16,512]{3,2,1,0:T(8,128)(2,1)} custom-call(s32[32]{0:T(128)} %order_ref.8, s32[2]{0:T(128)} %pad_add_fusion.ids_ref, f32[16,512]{1,0:T(8,128)} %amp_ref.3, bf16[32,16,16,512]{3,2,1,0:T(8,128)(2,1)} %refs_3_.3, bf16[32,16,16,512]{3,2,1,0:T(8,128)(2,1)} %refs_3_.3, bf16[32,16,16,512]{3,2,1,0:T(8,128)(2,1)} %refs_3_.3, ...), custom_call_target="tpu_custom_call" | custom-call | tf_op jit(solution)/shard_map/weigh/pallas_call | solution.py:68
  6.7 0.0 collective-permute-done.far_ref
  6.7 0.0 copy-start.1
  6.7 0.6 copy-done.1
  7.3 78.7 %draw.1.held_ref = bf16[96,512,1024]{2,1,0:T(8,128)(2,1)} custom-call(s32[8,512]{1,0:T(8,128)} %get-tuple-element.17.own_ref, s32[8,512]{1,0:T(8,128)} %copy-done.1), custom_call_target="tpu_custom_call" | custom-call | tf_op jit(solution)/shard_map/draw/pallas_call | solution.py:122
  86.1 8.7 %near.1.refs_0_ = bf16[128,16,1024]{2,1,0:T(8,128)(2,1)} custom-call(s32[2]{0:T(128)} %pad_add_fusion.ids_ref, s32[8,512]{1,0:T(8,128)} %get-tuple-element.17.own_ref, s32[8,512]{1,0:T(8,128)} %copy-done.1, bf16[128,16,512]{2,1,0:T(8,128)(2,1)} %bitcast.3.w_ref), custom_call_target="tpu_custom_call" | custom-call | tf_op jit(solution)/shard_map/near/pallas_call | solution.py:170
  94.7 4.6 %weigh.3 = bf16[16,8,16,512]{3,2,1,0:T(8,128)(2,1)} custom-call(s32[32]{0:T(128)} %order_ref.8, s32[2]{0:T(128)} %pad_add_fusion.ids_ref, f32[16,512]{1,0:T(8,128)} %amp_ref.3, bf16[32,16,16,512]{3,2,1,0:T(8,128)(2,1)} %refs_3_.3, bf16[32,16,16,512]{3,2,1,0:T(8,128)(2,1)} %refs_3_.3, bf16[32,16,16,512]{3,2,1,0:T(8,128)(2,1)} %refs_3_.3, ...), custom_call_target="tpu_custom_call" | custom-call | tf_op jit(solution)/shard_map/weigh/pallas_call | solution.py:68
  99.4 16.6 %all-to-all-start.1 = ((bf16[16,8,16,512]{3,2,1,0:T(8,128)(2,1)}), bf16[16,8,16,512]{3,2,1,0:T(8,128)(2,1)S(1)}, u32[]{:S(2)}, u32[]{:S(2)}) async-start(bf16[16,8,16,512]{3,2,1,0:T(8,128)(2,1)} %weigh.3), calls=%async_computation.1 | async-start | bytes 4194304 | tf_op jit(solution)/shard_map/all_to_all | solution.py:308
  116.0 0.0 collective-permute-start.1
  116.1 94.0 %all-to-all-done.1 = bf16[16,8,16,512]{3,2,1,0:T(8,128)(2,1)S(1)} async-done(((bf16[16,8,16,512]{3,2,1,0:T(8,128)(2,1)}), bf16[16,8,16,512]{3,2,1,0:T(8,128)(2,1)S(1)}, u32[]{:S(2)}, u32[]{:S(2)}) %all-to-all-start.1) | async-done | bytes 2097184 | tf_op jit(solution)/shard_map/all_to_all | solution.py:308
  210.1 9.5 %all-to-all-start = ((bf16[16,8,16,512]{3,2,1,0:T(8,128)(2,1)}), bf16[16,8,16,512]{3,2,1,0:T(8,128)(2,1)}, u32[]{:S(2)}, u32[]{:S(2)}) async-start(bf16[16,8,16,512]{3,2,1,0:T(8,128)(2,1)} %weigh.2), calls=%async_computation | async-start | bytes 4194304 | tf_op jit(solution)/shard_map/all_to_all | solution.py:308
  219.6 0.0 copy-done
  219.6 44.8 %finish.1 = (bf16[32,16,1024]{2,1,0:T(8,128)(2,1)}, bf16[96,16,1024]{2,1,0:T(8,128)(2,1)}) custom-call(s32[8,512]{1,0:T(8,128)} %get-tuple-element.17.own_ref, s32[8,512]{1,0:T(8,128)} %copy-done.1, bf16[128,16,512]{2,1,0:T(8,128)(2,1)} %bitcast.10, bf16[96,512,1024]{2,1,0:T(8,128)(2,1)} %draw.1.held_ref, bf16[128,16,512]{2,1,0:T(8,128)(2,1)} %bitcast.11), custom_call_target="tpu_custom_call" | custom-call | tf_op jit(solution)/shard_map/finish/pallas_call | solution.py:213
  264.4 49.5 %all-to-all-done = bf16[16,8,16,512]{3,2,1,0:T(8,128)(2,1)} async-done(((bf16[16,8,16,512]{3,2,1,0:T(8,128)(2,1)}), bf16[16,8,16,512]{3,2,1,0:T(8,128)(2,1)}, u32[]{:S(2)}, u32[]{:S(2)}) %all-to-all-start) | async-done | bytes 2097184 | tf_op jit(solution)/shard_map/all_to_all | solution.py:308
  313.9 98.1 %project.1 = bf16[128,16,1024]{2,1,0:T(8,128)(2,1)} custom-call(s32[2]{0:T(128)} %pad_add_fusion.ids_ref, s32[8,512]{1,0:T(8,128)} %get-tuple-element.17.own_ref, s32[8,512]{1,0:T(8,128)} %copy-done.1, bf16[128,16,512]{2,1,0:T(8,128)(2,1)} %bitcast.2.w_ref, bf16[128,16,1024]{2,1,0:T(8,128)(2,1)} %near.1.refs_0_), custom_call_target="tpu_custom_call", output_to_operand_aliasing={{}: (4, {})} | custom-call | tf_op jit(solution)/shard_map/project/pallas_call | solution.py:170
  412.0 0.0 collective-permute-done.1.far_ref
  412.0 11.6 %transform.3 = bf16[1,1536,512]{2,1,0:T(8,128)(2,1)} custom-call(s32[2]{0:T(128)} %pad_add_fusion.ids_ref, s32[32]{0:T(128)} %order_ref.8, s32[32]{0:T(128)} %counts_ref.3, bf16[2,768,4096]{2,1,0:T(8,128)(2,1)} %near_ref.3, bf16[2,768,4096]{2,1,0:T(8,128)(2,1)} %collective-permute-done.1.far_ref, bf16[2048,1024]{1,0:T(8,128)(2,1)} %bitcast.8, ...), custom_call_target="tpu_custom_call" | custom-call | tf_op jit(solution)/shard_map/transform/pallas_call | solution.py:278
  423.5 0.0 collective-permute-start.2
  423.5 11.6 %transform.2 = bf16[2,1536,512]{2,1,0:T(8,128)(2,1)} custom-call(s32[2]{0:T(128)} %pad_add_fusion.ids_ref, s32[32]{0:T(128)} %order_ref.8, s32[32]{0:T(128)} %counts_ref.3, bf16[2,768,4096]{2,1,0:T(8,128)(2,1)} %near_ref.3, bf16[2,768,4096]{2,1,0:T(8,128)(2,1)} %collective-permute-done.1.far_ref, bf16[2048,1024]{1,0:T(8,128)(2,1)} %bitcast.9, ...), custom_call_target="tpu_custom_call" | custom-call | tf_op jit(solution)/shard_map/transform/pallas_call | solution.py:278
  435.1 0.0 collective-permute-done.2
  435.1 1.2 constant_dynamic-update-slice_fusion
  (1 shorter events, 0.0 us)
Async XLA Ops:
  2.1 4.7 %collective-permute-start = (s32[8,512]{1,0:T(8,128)}, s32[8,512]{1,0:T(8,128)S(1)}, u32[]{:S(2)}, u32[]{:S(2)}) collective-permute-start(s32[8,512]{1,0:T(8,128)} %get-tuple-element.15), channel_id=1, source_target_pairs={{0,1},{1,0},{2,3},{3,2},{4,5},{5,4},{6,7},{7,6},{8,9},{9,8},{10,11... | collective-permute-start | bytes 49160 | tf_op jit(solution)/shard_map/ppermute | solution.py:305
  6.7 0.6 copy-start.1
  99.4 110.7 %all-to-all-start.1 = ((bf16[16,8,16,512]{3,2,1,0:T(8,128)(2,1)}), bf16[16,8,16,512]{3,2,1,0:T(8,128)(2,1)S(1)}, u32[]{:S(2)}, u32[]{:S(2)}) async-start(bf16[16,8,16,512]{3,2,1,0:T(8,128)(2,1)} %weigh.3), calls=%async_computation.1 | async-start | bytes 4194304 | tf_op jit(solution)/shard_map/all_to_all | solution.py:308
  116.0 295.9 %collective-permute-start.1 = (bf16[2,768,4096]{2,1,0:T(8,128)(2,1)}, bf16[2,768,4096]{2,1,0:T(8,128)(2,1)}, u32[]{:S(2)}, u32[]{:S(2)}) collective-permute-start(bf16[2,768,4096]{2,1,0:T(8,128)(2,1)} %near_ref.3), channel_id=1, source_target_pairs={{0,1},{1,0},{2,3},{3,2},{4,5},{5,4},{6,7},{7,6},{8,9},{9,8},{10,11... | collective-permute-start | bytes 37748744 | tf_op jit(solution)/shard_map/ppermute | solution.py:314
  210.1 9.5 %copy-start = (bf16[16,8,16,512]{3,2,1,0:T(8,128)(2,1)}, bf16[16,8,16,512]{3,2,1,0:T(8,128)(2,1)S(1)}, u32[]{:S(2)}) copy-start(bf16[16,8,16,512]{3,2,1,0:T(8,128)(2,1)S(1)} %all-to-all-done.1) | copy-start | bytes 6291460
  210.1 103.8 %all-to-all-start = ((bf16[16,8,16,512]{3,2,1,0:T(8,128)(2,1)}), bf16[16,8,16,512]{3,2,1,0:T(8,128)(2,1)}, u32[]{:S(2)}, u32[]{:S(2)}) async-start(bf16[16,8,16,512]{3,2,1,0:T(8,128)(2,1)} %weigh.2), calls=%async_computation | async-start | bytes 4194304 | tf_op jit(solution)/shard_map/all_to_all | solution.py:308
  423.5 11.6 %collective-permute-start.2 = (bf16[1,1536,512]{2,1,0:T(8,128)(2,1)}, bf16[1,1536,512]{2,1,0:T(8,128)(2,1)S(1)}, u32[]{:S(2)}, u32[]{:S(2)}) collective-permute-start(bf16[1,1536,512]{2,1,0:T(8,128)(2,1)} %transform.3), channel_id=1, source_target_pairs={{0,1},{1,0},{2,3},{3,2},{4,5},{5,4},{6,7},{7,6},{8,9},{9,8},{10,11... | collective-permute-start | bytes 4718600 | tf_op jit(solution)/shard_map/ppermute | solution.py:326

commit v3 on v2

--- a/solution.py
+++ b/solution.py
@@ -10,6 +10,7 @@
 
 golden = 1640531527
 tile = 256
+FULL = 63
 
 
 def wrap(value):
@@ -58,7 +59,7 @@
 def weigh(m_order, ids, singular_projection, noise_amp, part, chan):
     modes, pairs = singular_projection.shape[2:]
     count = m_order.shape[0] // 2
-    each = 4
+    each = 8
 
     def rows_of(place):
         return pl.BlockSpec(
@@ -74,7 +75,7 @@
             in_specs=[pl.BlockSpec((chan, pairs), lambda i, m, ids: (part, 0))] + [rows_of(k) for k in range(each)],
             out_specs=pl.BlockSpec((each, chan, modes, pairs), lambda i, m, ids: (i, 0, 0, 0)),
         ),
-        compiler_params=in_order(),
+        compiler_params=in_order(FULL),
         name="weigh",
     )(m_order, ids, noise_amp, *[singular_projection] * each)
 
@@ -125,7 +126,7 @@
         grid=(count // each,),
         in_specs=[seed_spec(s) for s in seeds],
         out_specs=pl.BlockSpec((each, pairs, reals), lambda i: (i, 0, 0)),
-        compiler_params=in_order(60),
+        compiler_params=in_order(FULL),
         name="draw",
     )(*seeds)
 
@@ -177,14 +178,36 @@
             out_specs=pl.BlockSpec((each, modes, reals), at),
         ),
         input_output_aliases=aliases,
-        compiler_params=in_order(60),
+        compiler_params=in_order(FULL),
         name="near" if local else "project",
     )(*operands)
 
 
-def finish_body(own_ref, far_ref, w_ref, held_ref, held_w_ref, out_ref, held_out_ref, *, first, half, chan):
+def turn(step, steps, fetch):
+    @pl.when(step == 0)
+    def _():
+        for ahead in range(2):
+            fetch(ahead, ahead, True)
+
+    @pl.when(step + 2 < steps)
+    def _():
+        fetch(step + 2, lax.rem(step + 2, 3), True)
+
+    slot = lax.rem(step, 3)
+    fetch(step, slot, False)
+    return slot
+
+
+def finish_body(own_ref, far_ref, w_ref, held_hbm, held_w_ref, out_ref, held_out_ref, ring_ref, sems, *, first, half, chan):
     each, _, pairs = w_ref.shape
-    held_each = held_ref.shape[0] // each
+    step_held = ring_ref.shape[1]
+    held_each = step_held // each
+
+    def fetch(step, slot, start):
+        copy = pltpu.make_async_copy(held_hbm.at[pl.ds(step * step_held, step_held)], ring_ref.at[slot], sems.at[slot])
+        copy.start() if start else copy.wait()
+
+    slot = turn(pl.program_id(0), held_hbm.shape[0] // step_held, fetch)
     for place in range(each):
         channel = channel_of(first + pl.program_id(0) * each + place, half, chan)
         w = w_ref[place]
@@ -197,7 +220,7 @@
         for r0, b0, draws in draw_tiles((own_ref, far_ref), channel, pairs):
             total = put_product(w, draws, r0, b0, pairs, total, centre, out_ref, place)
             for n, k in enumerate(kept):
-                old = held_ref[k, b0 : b0 + tile, r0 : r0 + tile]
+                old = ring_ref[slot, k, b0 : b0 + tile, r0 : r0 + tile]
                 held_total[n] = put_product(
                     held_w[n], old, r0, b0, pairs, held_total[n], held_centre[n], held_out_ref, k
                 )
@@ -220,43 +243,61 @@
         in_specs=[seed_spec(s) for s in seeds]
         + [
             pl.BlockSpec((each, modes, pairs), lambda i: (first // each + i, 0, 0)),
-            pl.BlockSpec((held_each, pairs, reals), lambda i: (i, 0, 0)),
+            pl.BlockSpec(memory_space=pl.ANY),
             pl.BlockSpec((held_each, modes, pairs), lambda i: (i, 0, 0)),
         ],
         out_specs=[
             pl.BlockSpec((each, modes, reals), lambda i: (i, 0, 0)),
             pl.BlockSpec((held_each, modes, reals), lambda i: (i, 0, 0)),
         ],
-        compiler_params=in_order(60),
+        scratch_shapes=[pltpu.VMEM((3, held_each, pairs, reals), held.dtype), pltpu.SemaphoreType.DMA((3,))],
+        compiler_params=in_order(FULL),
         name="finish",
     )(*seeds, weights, held, weights)
 
 
-def transform_body(ids_ref, order_ref, counts_ref, near_ref, far_ref, *refs, rows, blocks, modes):
-    vec_refs, out_ref = refs[:-1], refs[-1]
+def transform_body(ids_ref, order_ref, counts_ref, near_hbm, far_hbm, *refs, modes):
+    *vec_refs, out_ref, ring_ref, sems = refs
     step = pl.program_id(0)
+    rows = ring_ref.shape[1]
+    blocks = near_hbm.shape[1] // rows
+    core = ids_ref[1]
+    limit = counts_ref[order_ref[2 * ids_ref[0] + core]]
+
+    def fetch(step, slot, start):
+        block = step if isinstance(step, int) else lax.rem(step, blocks)
+
+        def copy_from(ref):
+            return pltpu.make_async_copy(ref.at[core, pl.ds(block * rows, rows)], ring_ref.at[slot], sems.at[slot])
+
+        if not start:
+            copy_from(near_hbm).wait()
+            return
+        mine = core == step // blocks
+
+        @pl.when(mine)
+        def _():
+            copy_from(near_hbm).start()
+
+        @pl.when(jnp.logical_not(mine))
+        def _():
+            copy_from(far_hbm).start()
+
+    slot = turn(step, 2 * blocks, fetch)
     first = step * rows
-    limit = counts_ref[order_ref[2 * ids_ref[0] + ids_ref[1]]]
-    mine = step // blocks == ids_ref[1]
-
-    def run(kl_ref):
+
+    @pl.when(first < limit)
+    def _():
         total = None
         lead, *trail = vec_refs
         at = [(ref, k) for ref in trail for k in range(0, ref.shape[0], modes)]
         for k, (ref, start) in enumerate(at):
             piece = jnp.concatenate([lead[k * modes : (k + 1) * modes, :], ref[start : start + modes, :]], 0)
-            part = jnp.dot(kl_ref[0, :, 2 * k * modes : 2 * (k + 1) * modes], piece, preferred_element_type=jnp.float32)
+            columns = ring_ref[slot, :, 2 * k * modes : 2 * (k + 1) * modes]
+            part = jnp.dot(columns, piece, preferred_element_type=jnp.float32)
             total = part if total is None else total + part
         row = first + lax.broadcasted_iota(jnp.int32, total.shape, 0)
         out_ref[0] = jnp.where(row < limit, total, 0.0).astype(jnp.bfloat16)
-
-    @pl.when((first < limit) & mine)
-    def _():
-        run(near_ref)
-
-    @pl.when((first < limit) & jnp.logical_not(mine))
-    def _():
-        run(far_ref)
 
     @pl.when(first >= limit)
     def _():
@@ -267,28 +308,21 @@
     held, length = kl_near.shape[1:]
     reals = vectors[0].shape[1] // halves
     rows = 256
-    blocks = held // rows
-
-    def near(i, s, o, c):
-        return (s[1], jnp.clip(i - s[1] * blocks, 0, blocks - 1), 0)
-
-    def far(i, s, o, c):
-        return (s[1], jnp.clip(i - (1 - s[1]) * blocks, 0, blocks - 1), 0)
-
-    return pl.pallas_call(
-        functools.partial(transform_body, rows=rows, blocks=blocks, modes=modes),
+    return pl.pallas_call(
+        functools.partial(transform_body, modes=modes),
         out_shape=jax.ShapeDtypeStruct((slots, 2 * held, reals), jnp.bfloat16),
         grid_spec=pltpu.PrefetchScalarGridSpec(
             num_scalar_prefetch=3,
-            grid=(2 * blocks,),
+            grid=(2 * held // rows,),
             in_specs=[
-                pl.BlockSpec((1, rows, length), near),
-                pl.BlockSpec((1, rows, length), far),
+                pl.BlockSpec(memory_space=pl.ANY),
+                pl.BlockSpec(memory_space=pl.ANY),
                 *[pl.BlockSpec((v.shape[0], reals), lambda i, s, o, c: (0, half)) for v in vectors],
             ],
             out_specs=pl.BlockSpec((1, rows, reals), lambda i, s, o, c: (s[1] * (slots - 1), i, 0)),
+            scratch_shapes=[pltpu.VMEM((3, rows, length), kl_near.dtype), pltpu.SemaphoreType.DMA((3,))],
         ),
-        compiler_params=in_order(60),
+        compiler_params=in_order(FULL),
         name="transform",
     )(ids, m_order, mode_counts, kl_near, kl_far, *vectors)
 

time: 443 us -> 442 us (level)
  Pallas kernels: 264 us -> 256 us
    all_to_all x2, waiting for transfers between devices: 144 us -> 148 us  [exchange(): lax.all_to_all(sent, 'freq', split_axis=0, concat_axis=0, tiled=True)]
    pallas_call x1, Pallas kernels: 44.8 us -> 40.2 us  [finish(): pl.pallas_call(functools.partial(finish_body, first=first, half=half, cha...]
  transfers between devices with their start and end apart: 5 -> 5, of which waited for: 2 -> 2; matrix products, arithmetic and copies ran while one was open for 0% -> 0% of each run, Pallas kernels for 36% -> 35%
where the time goes in v3:
time: 442 us; the launch traced here: 435 us
  Pallas kernels  256 us (58%)
  waiting for transfers between devices  148 us (33%)
  starting transfers between devices  26.3 us (6%)
    all_to_all x2, waiting for transfers between devices, exchange(): lax.all_to_all(sent, 'freq', split_axis=0, concat_axis=0, tiled=True)  148 us
    pallas_call x2, Pallas kernels, project(): pl.pallas_call(functools.partial(project_body, half=half, chan=chan, loca...  107 us
    pallas_call x1, Pallas kernels, draw(): pl.pallas_call(functools.partial(draw_body, first=first, half=half, chan=...  78.7 us
    pallas_call x1, Pallas kernels, finish(): pl.pallas_call(functools.partial(finish_body, first=first, half=half, cha...  40.2 us
    all_to_all x2, starting transfers between devices, exchange(): lax.all_to_all(sent, 'freq', split_axis=0, concat_axis=0, tiled=True)  26.1 us
    pallas_call x2, Pallas kernels, transform(): pl.pallas_call(functools.partial(transform_body, modes=modes), out_shape=...  22.1 us
  transfers between devices with their start and end apart: 5, of which 2 were waited for; matrix products, arithmetic and copies ran while one was open for 0% of the time, Pallas kernels for 35%

profile of v3, /device:TPU:214, one launch (start us, length us, event | category | flops | bytes accessed | tf_op | source)
XLA Modules:
  0.0 434.7 jit_solution(2512267493122020390)
XLA Ops:
  0.0 0.6 pad_add_fusion.ids_ref
  0.6 1.5 pick.1
  2.1 0.0 collective-permute-start
  2.1 3.5 weigh.2
  5.6 0.0 collective-permute-done.far_ref
  5.6 0.0 copy-start
  5.6 0.6 copy-done
  6.2 78.7 %draw.1.held_hbm = bf16[96,512,1024]{2,1,0:T(8,128)(2,1)} custom-call(s32[8,512]{1,0:T(8,128)} %get-tuple-element.17.own_ref, s32[8,512]{1,0:T(8,128)} %copy-done), custom_call_target="tpu_custom_call" | custom-call | tf_op jit(solution)/shard_map/draw/pallas_call | solution.py:123
  84.9 8.7 %near.1.refs_0_ = bf16[128,16,1024]{2,1,0:T(8,128)(2,1)} custom-call(s32[2]{0:T(128)} %pad_add_fusion.ids_ref, s32[8,512]{1,0:T(8,128)} %get-tuple-element.17.own_ref, s32[8,512]{1,0:T(8,128)} %copy-done, bf16[128,16,512]{2,1,0:T(8,128)(2,1)} %bitcast.3.w_ref), custom_call_target="tpu_custom_call" | custom-call | tf_op jit(solution)/shard_map/near/pallas_call | solution.py:171
  93.6 3.5 weigh.3
  97.1 16.6 %all-to-all-start.1 = ((bf16[16,8,16,512]{3,2,1,0:T(8,128)(2,1)}), bf16[16,8,16,512]{3,2,1,0:T(8,128)(2,1)}, u32[]{:S(2)}, u32[]{:S(2)}) async-start(bf16[16,8,16,512]{3,2,1,0:T(8,128)(2,1)} %weigh.3), calls=%async_computation.1 | async-start | bytes 4194304 | tf_op jit(solution)/shard_map/all_to_all | solution.py:342
  113.8 0.0 collective-permute-start.1
  113.8 94.1 %all-to-all-done.1 = bf16[16,8,16,512]{3,2,1,0:T(8,128)(2,1)} async-done(((bf16[16,8,16,512]{3,2,1,0:T(8,128)(2,1)}), bf16[16,8,16,512]{3,2,1,0:T(8,128)(2,1)}, u32[]{:S(2)}, u32[]{:S(2)}) %all-to-all-start.1) | async-done | bytes 2097184 | tf_op jit(solution)/shard_map/all_to_all | solution.py:342
  207.9 9.5 %all-to-all-start = ((bf16[16,8,16,512]{3,2,1,0:T(8,128)(2,1)}), bf16[16,8,16,512]{3,2,1,0:T(8,128)(2,1)}, u32[]{:S(2)}, u32[]{:S(2)}) async-start(bf16[16,8,16,512]{3,2,1,0:T(8,128)(2,1)} %weigh.2), calls=%async_computation | async-start | bytes 4194304 | tf_op jit(solution)/shard_map/all_to_all | solution.py:342
  217.4 40.2 %finish.1 = (bf16[32,16,1024]{2,1,0:T(8,128)(2,1)}, bf16[96,16,1024]{2,1,0:T(8,128)(2,1)}) custom-call(s32[8,512]{1,0:T(8,128)} %get-tuple-element.17.own_ref, s32[8,512]{1,0:T(8,128)} %copy-done, bf16[128,16,512]{2,1,0:T(8,128)(2,1)} %bitcast.5.w_ref.held_w_ref, bf16[96,512,1024]{2,1,0:T(8,128)(2,1)} %draw.1.held_hbm, ...), custom_call_target="tpu_custom_call" | custom-call | tf_op jit(solution)/shard_map/finish/pallas_call | solution.py:236
  257.6 54.1 %all-to-all-done = bf16[16,8,16,512]{3,2,1,0:T(8,128)(2,1)} async-done(((bf16[16,8,16,512]{3,2,1,0:T(8,128)(2,1)}), bf16[16,8,16,512]{3,2,1,0:T(8,128)(2,1)}, u32[]{:S(2)}, u32[]{:S(2)}) %all-to-all-start) | async-done | bytes 2097184 | tf_op jit(solution)/shard_map/all_to_all | solution.py:342
  311.7 98.1 %project.1 = bf16[128,16,1024]{2,1,0:T(8,128)(2,1)} custom-call(s32[2]{0:T(128)} %pad_add_fusion.ids_ref, s32[8,512]{1,0:T(8,128)} %get-tuple-element.17.own_ref, s32[8,512]{1,0:T(8,128)} %copy-done, bf16[128,16,512]{2,1,0:T(8,128)(2,1)} %bitcast.2.w_ref, bf16[128,16,1024]{2,1,0:T(8,128)(2,1)} %near.1.refs_0_), custom_call_target="tpu_custom_call", output_to_operand_aliasing={{}: (4, {})} | custom-call | tf_op jit(solution)/shard_map/project/pallas_call | solution.py:171
  409.8 0.0 collective-permute-done.1.far_hbm
  409.8 11.0 %transform.3 = bf16[1,1536,512]{2,1,0:T(8,128)(2,1)} custom-call(s32[2]{0:T(128)} %pad_add_fusion.ids_ref, s32[32]{0:T(128)} %order_ref.8, s32[32]{0:T(128)} %counts_ref.3, bf16[2,768,4096]{2,1,0:T(8,128)(2,1)} %near_hbm.3, bf16[2,768,4096]{2,1,0:T(8,128)(2,1)} %collective-permute-done.1.far_hbm, bf16[2048,1024]{1,0:T(8,128)(2,1)} %bitcast.8, ...), custom_call_target="tpu_custom_call" | custom-call | tf_op jit(solution)/shard_map/transform/pallas_call | solution.py:311
  420.8 0.1 collective-permute-start.2
  421.0 11.0 %transform.2 = bf16[2,1536,512]{2,1,0:T(8,128)(2,1)} custom-call(s32[2]{0:T(128)} %pad_add_fusion.ids_ref, s32[32]{0:T(128)} %order_ref.8, s32[32]{0:T(128)} %counts_ref.3, bf16[2,768,4096]{2,1,0:T(8,128)(2,1)} %near_hbm.3, bf16[2,768,4096]{2,1,0:T(8,128)(2,1)} %collective-permute-done.1.far_hbm, bf16[2048,1024]{1,0:T(8,128)(2,1)} %bitcast.9, ...), custom_call_target="tpu_custom_call" | custom-call | tf_op jit(solution)/shard_map/transform/pallas_call | solution.py:311
  432.0 0.0 collective-permute-done.2
  432.0 2.7 constant_dynamic-update-slice_fusion
Async XLA Ops:
  2.1 3.5 collective-permute-start
  5.6 0.6 copy-start
  97.1 110.8 %all-to-all-start.1 = ((bf16[16,8,16,512]{3,2,1,0:T(8,128)(2,1)}), bf16[16,8,16,512]{3,2,1,0:T(8,128)(2,1)}, u32[]{:S(2)}, u32[]{:S(2)}) async-start(bf16[16,8,16,512]{3,2,1,0:T(8,128)(2,1)} %weigh.3), calls=%async_computation.1 | async-start | bytes 4194304 | tf_op jit(solution)/shard_map/all_to_all | solution.py:342
  113.8 296.0 %collective-permute-start.1 = (bf16[2,768,4096]{2,1,0:T(8,128)(2,1)}, bf16[2,768,4096]{2,1,0:T(8,128)(2,1)}, u32[]{:S(2)}, u32[]{:S(2)}) collective-permute-start(bf16[2,768,4096]{2,1,0:T(8,128)(2,1)} %near_hbm.3), channel_id=1, source_target_pairs={{0,1},{1,0},{2,3},{3,2},{4,5},{5,4},{6,7},{7,6},{8,9},{9,8},{10,11... | collective-permute-start | bytes 37748744 | tf_op jit(solution)/shard_map/ppermute | solution.py:348
  207.9 103.8 %all-to-all-start = ((bf16[16,8,16,512]{3,2,1,0:T(8,128)(2,1)}), bf16[16,8,16,512]{3,2,1,0:T(8,128)(2,1)}, u32[]{:S(2)}, u32[]{:S(2)}) async-start(bf16[16,8,16,512]{3,2,1,0:T(8,128)(2,1)} %weigh.2), calls=%async_computation | async-start | bytes 4194304 | tf_op jit(solution)/shard_map/all_to_all | solution.py:342
  420.8 11.2 %collective-permute-start.2 = (bf16[1,1536,512]{2,1,0:T(8,128)(2,1)}, bf16[1,1536,512]{2,1,0:T(8,128)(2,1)}, u32[]{:S(2)}, u32[]{:S(2)}) collective-permute-start(bf16[1,1536,512]{2,1,0:T(8,128)(2,1)} %transform.3), channel_id=1, source_target_pairs={{0,1},{1,0},{2,3},{3,2},{4,5},{5,4},{6,7},{7,6},{8,9},{9,8},{10,11... | collective-permute-start | bytes 4718600 | tf_op jit(solution)/shard_map/ppermute | solution.py:360

commit v4 on v3

--- a/solution.py
+++ b/solution.py
@@ -256,8 +256,10 @@
     )(*seeds, weights, held, weights)
 
 
-def transform_body(ids_ref, order_ref, counts_ref, near_hbm, far_hbm, *refs, modes):
-    *vec_refs, out_ref, ring_ref, sems = refs
+def transform_body(ids_ref, order_ref, counts_ref, near_hbm, far_hbm, *refs, modes, half):
+    count = (len(refs) - 4) // 2
+    vec_hbm, out_ref, vec_refs = refs[:count], refs[count], refs[count + 1 : 2 * count + 1]
+    ring_ref, sems, vec_sems = refs[2 * count + 1 :]
     step = pl.program_id(0)
     rows = ring_ref.shape[1]
     blocks = near_hbm.shape[1] // rows
@@ -283,7 +285,23 @@
         def _():
             copy_from(far_hbm).start()
 
+    def vectors():
+        for n, (src, dst) in enumerate(zip(vec_hbm, vec_refs)):
+            reals = dst.shape[1]
+            yield pltpu.make_async_copy(src.at[:, pl.ds(half * reals, reals)], dst, vec_sems.at[n])
+
+    @pl.when(step == 0)
+    def _():
+        for copy in vectors():
+            copy.start()
+
     slot = turn(step, 2 * blocks, fetch)
+
+    @pl.when(step == 0)
+    def _():
+        for copy in vectors():
+            copy.wait()
+
     first = step * rows
 
     @pl.when(first < limit)
@@ -309,7 +327,7 @@
     reals = vectors[0].shape[1] // halves
     rows = 256
     return pl.pallas_call(
-        functools.partial(transform_body, modes=modes),
+        functools.partial(transform_body, modes=modes, half=half),
         out_shape=jax.ShapeDtypeStruct((slots, 2 * held, reals), jnp.bfloat16),
         grid_spec=pltpu.PrefetchScalarGridSpec(
             num_scalar_prefetch=3,
@@ -317,12 +335,17 @@
             in_specs=[
                 pl.BlockSpec(memory_space=pl.ANY),
                 pl.BlockSpec(memory_space=pl.ANY),
-                *[pl.BlockSpec((v.shape[0], reals), lambda i, s, o, c: (0, half)) for v in vectors],
+                *[pl.BlockSpec(memory_space=pl.ANY) for v in vectors],
             ],
             out_specs=pl.BlockSpec((1, rows, reals), lambda i, s, o, c: (s[1] * (slots - 1), i, 0)),
-            scratch_shapes=[pltpu.VMEM((3, rows, length), kl_near.dtype), pltpu.SemaphoreType.DMA((3,))],
+            scratch_shapes=[
+                *[pltpu.VMEM((v.shape[0], reals), v.dtype) for v in vectors],
+                pltpu.VMEM((3, rows, length), kl_near.dtype),
+                pltpu.SemaphoreType.DMA((3,)),
+                pltpu.SemaphoreType.DMA((len(vectors),)),
+            ],
         ),
-        compiler_params=in_order(FULL),
+        compiler_params=in_order(60),
         name="transform",
     )(ids, m_order, mode_counts, kl_near, kl_far, *vectors)
 

time: 442 us -> 439 us (level)
  no operation moved by 1% of the time
where the time goes in v4:
time: 439 us; the launch traced here: 433 us
  Pallas kernels  256 us (58%)
  waiting for transfers between devices  148 us (34%)
  starting transfers between devices  26.3 us (6%)
    all_to_all x2, waiting for transfers between devices, exchange(): lax.all_to_all(sent, 'freq', split_axis=0, concat_axis=0, tiled=True)  148 us
    pallas_call x2, Pallas kernels, project(): pl.pallas_call(functools.partial(project_body, half=half, chan=chan, loca...  107 us
    pallas_call x1, Pallas kernels, draw(): pl.pallas_call(functools.partial(draw_body, first=first, half=half, chan=...  78.7 us
    pallas_call x1, Pallas kernels, finish(): pl.pallas_call(functools.partial(finish_body, first=first, half=half, cha...  40.2 us
    all_to_all x2, starting transfers between devices, exchange(): lax.all_to_all(sent, 'freq', split_axis=0, concat_axis=0, tiled=True)  26.1 us
    pallas_call x2, Pallas kernels, transform(): pl.pallas_call(functools.partial(transform_body, modes=modes, half=half),...  21.3 us
  transfers between devices with their start and end apart: 5, of which 2 were waited for; matrix products, arithmetic and copies ran while one was open for 0% of the time, Pallas kernels for 35%

profile of v4, /device:TPU:214, one launch (start us, length us, event | category | flops | bytes accessed | tf_op | source)
XLA Modules:
  0.0 432.6 jit_solution(15838011523540923018)
XLA Ops:
  0.0 0.6 pad_add_fusion.ids_ref
  0.6 1.5 pick.1
  2.1 0.0 collective-permute-start
  2.1 3.5 weigh.2
  5.6 0.0 collective-permute-done.far_ref
  5.6 0.0 copy-start
  5.6 0.6 copy-done
  6.2 78.7 %draw.1.held_hbm = bf16[96,512,1024]{2,1,0:T(8,128)(2,1)} custom-call(s32[8,512]{1,0:T(8,128)} %get-tuple-element.17.own_ref, s32[8,512]{1,0:T(8,128)} %copy-done), custom_call_target="tpu_custom_call" | custom-call | tf_op jit(solution)/shard_map/draw/pallas_call | solution.py:123
  84.9 8.7 %near.1.refs_0_ = bf16[128,16,1024]{2,1,0:T(8,128)(2,1)} custom-call(s32[2]{0:T(128)} %pad_add_fusion.ids_ref, s32[8,512]{1,0:T(8,128)} %get-tuple-element.17.own_ref, s32[8,512]{1,0:T(8,128)} %copy-done, bf16[128,16,512]{2,1,0:T(8,128)(2,1)} %bitcast.3.w_ref), custom_call_target="tpu_custom_call" | custom-call | tf_op jit(solution)/shard_map/near/pallas_call | solution.py:171
  93.6 3.5 weigh.3
  97.1 16.6 %all-to-all-start.1 = ((bf16[16,8,16,512]{3,2,1,0:T(8,128)(2,1)}), bf16[16,8,16,512]{3,2,1,0:T(8,128)(2,1)}, u32[]{:S(2)}, u32[]{:S(2)}) async-start(bf16[16,8,16,512]{3,2,1,0:T(8,128)(2,1)} %weigh.3), calls=%async_computation.1 | async-start | bytes 4194304 | tf_op jit(solution)/shard_map/all_to_all | solution.py:365
  113.8 0.0 collective-permute-start.1
  113.8 94.1 %all-to-all-done.1 = bf16[16,8,16,512]{3,2,1,0:T(8,128)(2,1)} async-done(((bf16[16,8,16,512]{3,2,1,0:T(8,128)(2,1)}), bf16[16,8,16,512]{3,2,1,0:T(8,128)(2,1)}, u32[]{:S(2)}, u32[]{:S(2)}) %all-to-all-start.1) | async-done | bytes 2097184 | tf_op jit(solution)/shard_map/all_to_all | solution.py:365
  207.9 9.5 %all-to-all-start = ((bf16[16,8,16,512]{3,2,1,0:T(8,128)(2,1)}), bf16[16,8,16,512]{3,2,1,0:T(8,128)(2,1)}, u32[]{:S(2)}, u32[]{:S(2)}) async-start(bf16[16,8,16,512]{3,2,1,0:T(8,128)(2,1)} %weigh.2), calls=%async_computation | async-start | bytes 4194304 | tf_op jit(solution)/shard_map/all_to_all | solution.py:365
  217.4 40.2 %finish.1 = (bf16[32,16,1024]{2,1,0:T(8,128)(2,1)}, bf16[96,16,1024]{2,1,0:T(8,128)(2,1)}) custom-call(s32[8,512]{1,0:T(8,128)} %get-tuple-element.17.own_ref, s32[8,512]{1,0:T(8,128)} %copy-done, bf16[128,16,512]{2,1,0:T(8,128)(2,1)} %bitcast.5.w_ref.held_w_ref, bf16[96,512,1024]{2,1,0:T(8,128)(2,1)} %draw.1.held_hbm, ...), custom_call_target="tpu_custom_call" | custom-call | tf_op jit(solution)/shard_map/finish/pallas_call | solution.py:236
  257.6 54.1 %all-to-all-done = bf16[16,8,16,512]{3,2,1,0:T(8,128)(2,1)} async-done(((bf16[16,8,16,512]{3,2,1,0:T(8,128)(2,1)}), bf16[16,8,16,512]{3,2,1,0:T(8,128)(2,1)}, u32[]{:S(2)}, u32[]{:S(2)}) %all-to-all-start) | async-done | bytes 2097184 | tf_op jit(solution)/shard_map/all_to_all | solution.py:365
  311.7 98.1 %project.1 = bf16[128,16,1024]{2,1,0:T(8,128)(2,1)} custom-call(s32[2]{0:T(128)} %pad_add_fusion.ids_ref, s32[8,512]{1,0:T(8,128)} %get-tuple-element.17.own_ref, s32[8,512]{1,0:T(8,128)} %copy-done, bf16[128,16,512]{2,1,0:T(8,128)(2,1)} %bitcast.2.w_ref, bf16[128,16,1024]{2,1,0:T(8,128)(2,1)} %near.1.refs_0_), custom_call_target="tpu_custom_call", output_to_operand_aliasing={{}: (4, {})} | custom-call | tf_op jit(solution)/shard_map/project/pallas_call | solution.py:171
  409.8 0.0 collective-permute-done.1.far_hbm
  409.8 10.6 %transform.3 = bf16[1,1536,512]{2,1,0:T(8,128)(2,1)} custom-call(s32[2]{0:T(128)} %pad_add_fusion.ids_ref, s32[32]{0:T(128)} %order_ref.8, s32[32]{0:T(128)} %counts_ref.3, bf16[2,768,4096]{2,1,0:T(8,128)(2,1)} %near_hbm.3, bf16[2,768,4096]{2,1,0:T(8,128)(2,1)} %collective-permute-done.1.far_hbm, bf16[2048,1024]{1,0:T(8,128)(2,1)} %bitcast.8, ...), custom_call_target="tpu_custom_call" | custom-call | tf_op jit(solution)/shard_map/transform/pallas_call | solution.py:329
  420.5 0.1 collective-permute-start.2
  420.6 10.7 %transform.2 = bf16[2,1536,512]{2,1,0:T(8,128)(2,1)} custom-call(s32[2]{0:T(128)} %pad_add_fusion.ids_ref, s32[32]{0:T(128)} %order_ref.8, s32[32]{0:T(128)} %counts_ref.3, bf16[2,768,4096]{2,1,0:T(8,128)(2,1)} %near_hbm.3, bf16[2,768,4096]{2,1,0:T(8,128)(2,1)} %collective-permute-done.1.far_hbm, bf16[2048,1024]{1,0:T(8,128)(2,1)} %bitcast.9, ...), custom_call_target="tpu_custom_call" | custom-call | tf_op jit(solution)/shard_map/transform/pallas_call | solution.py:329
  431.3 0.0 collective-permute-done.2
  431.3 1.3 constant_dynamic-update-slice_fusion
Async XLA Ops:
  2.1 3.5 collective-permute-start
  5.6 0.6 copy-start
  97.1 110.8 %all-to-all-start.1 = ((bf16[16,8,16,512]{3,2,1,0:T(8,128)(2,1)}), bf16[16,8,16,512]{3,2,1,0:T(8,128)(2,1)}, u32[]{:S(2)}, u32[]{:S(2)}) async-start(bf16[16,8,16,512]{3,2,1,0:T(8,128)(2,1)} %weigh.3), calls=%async_computation.1 | async-start | bytes 4194304 | tf_op jit(solution)/shard_map/all_to_all | solution.py:365
  113.8 296.0 %collective-permute-start.1 = (bf16[2,768,4096]{2,1,0:T(8,128)(2,1)}, bf16[2,768,4096]{2,1,0:T(8,128)(2,1)}, u32[]{:S(2)}, u32[]{:S(2)}) collective-permute-start(bf16[2,768,4096]{2,1,0:T(8,128)(2,1)} %near_hbm.3), channel_id=1, source_target_pairs={{0,1},{1,0},{2,3},{3,2},{4,5},{5,4},{6,7},{7,6},{8,9},{9,8},{10,11... | collective-permute-start | bytes 37748744 | tf_op jit(solution)/shard_map/ppermute | solution.py:371
  207.9 103.8 %all-to-all-start = ((bf16[16,8,16,512]{3,2,1,0:T(8,128)(2,1)}), bf16[16,8,16,512]{3,2,1,0:T(8,128)(2,1)}, u32[]{:S(2)}, u32[]{:S(2)}) async-start(bf16[16,8,16,512]{3,2,1,0:T(8,128)(2,1)} %weigh.2), calls=%async_computation | async-start | bytes 4194304 | tf_op jit(solution)/shard_map/all_to_all | solution.py:365
  420.5 10.8 %collective-permute-start.2 = (bf16[1,1536,512]{2,1,0:T(8,128)(2,1)}, bf16[1,1536,512]{2,1,0:T(8,128)(2,1)S(1)}, u32[]{:S(2)}, u32[]{:S(2)}) collective-permute-start(bf16[1,1536,512]{2,1,0:T(8,128)(2,1)} %transform.3), channel_id=1, source_target_pairs={{0,1},{1,0},{2,3},{3,2},{4,5},{5,4},{6,7},{7,6},{8,9},{9,8},{10,11... | collective-permute-start | bytes 4718600 | tf_op jit(solution)/shard_map/ppermute | solution.py:383
